TPU v7x, 32 devices: a whole 2x2x4 slice. The times are simulated.
32 devices in a mesh: gx: 4 (over x, core), gy: 4 (over z), gz: 2 (over y).
Axes of the slice: x: 2, y: 2, z: 4, core: 2. Of those that a mesh axis runs over, the one named last changes fastest.
Arguments:
- velocity: float32 [3, 64, 128, 256], P(None, 'gx', 'gy', 'gz'), may hold values from -4 to 4
- plane_early: float32 [3, 128, 256], P(None, 'gy', 'gx'), may hold values from -4 to 4
- plane_late: float32 [3, 128, 256], P(None, 'gy', 'gx'), may hold values from -4 to 4
- blend: float32 [1], replicated, may hold values from 0 to 1
Outputs:
- advanced: float32 [3, 64, 128, 256], P(None, 'gx', 'gy', 'gz')
All inputs are finite; a program needn't handle non-finite values.
Results may differ from a plain program's by a relative error of at most 0.00002.
Values sent between devices are 32-bit elements; how exact they have to be, the bound alone decides.
A program may use at most 64 MiB of HBM per device.

v0:
```python
import functools

import jax
import jax.numpy as jnp
from jax import lax
from jax.experimental import pallas as pl
from jax.experimental.pallas import tpu as pltpu
from jax.sharding import PartitionSpec as P

STEPS = 4
COURANT = 0.08
UNROLL = 7
TOP = 8

MESH = pl.DeviceIdType.MESH


def kernel(sizes, vel_hbm, early_hbm, late_hbm, blend_ref, out_ref,
           cur, early, late, inflow_send, inflow_recv,
           y_send, y_recv, z_send, z_low, z_high,
           load_sem, xs, xr, ys, yr, zs, zr, fs, fr):
    nx, ny, nz = sizes
    comps, cells_x, cells_y, cells_z = vel_hbm.shape
    share = nx // nz
    piece = early_hbm.shape[2]
    gx, gy, gz = (lax.axis_index(name) for name in ("gx", "gy", "gz"))
    own = pl.ds(TOP, cells_y)

    load_v = pltpu.make_async_copy(
        vel_hbm, cur.at[0, :, pl.ds(1, cells_x), own, :], load_sem.at[0])
    load_e = pltpu.make_async_copy(early_hbm, early, load_sem.at[1])
    load_l = pltpu.make_async_copy(late_hbm, late, load_sem.at[2])
    load_e.start()
    load_l.start()
    load_v.start()

    has_left, has_right = gx > 0, gx < nx - 1
    has_below, has_above = gz > 0, gz < nz - 1
    feeds = (gz == gx // share) & (gx != 0)
    y_up = {"gy": lax.rem(gy + 1, ny)}
    y_down = {"gy": lax.rem(gy + ny - 1, ny)}

    barrier = pltpu.get_barrier_semaphore()
    peers = [
        (has_left, {"gx": gx - 1}),
        (has_right, {"gx": gx + 1}),
        (has_below, {"gz": gz - 1}),
        (has_above, {"gz": gz + 1}),
        (feeds, {"gx": 0}),
    ]
    for k in range(share):
        source = gz * share + k
        peers.append(((gx == 0) & (source != 0), {"gx": source}))
    expected = jnp.int32(2)
    for where in (y_up, y_down):
        pl.semaphore_signal(barrier, 1, device_id=where, device_id_type=MESH)
    for present, where in peers:
        @pl.when(present)
        def _(where=where):
            pl.semaphore_signal(barrier, 1, device_id=where, device_id_type=MESH)
        expected = expected + jnp.where(present, 1, 0)

    def remote(src, dst, send, recv, where):
        return pltpu.make_async_remote_copy(
            src_ref=src, dst_ref=dst, send_sem=send, recv_sem=recv,
            device_id=where, device_id_type=MESH)

    def x_copies(t):
        return [
            (has_right, has_left, remote(
                cur.at[t, :, cells_x, own, :], cur.at[t, :, 0, own, :],
                xs.at[t, 0], xr.at[t, 0], {"gx": gx + 1})),
            (has_left, has_right, remote(
                cur.at[t, :, 1, own, :], cur.at[t, :, cells_x + 1, own, :],
                xs.at[t, 1], xr.at[t, 1], {"gx": gx - 1})),
        ]

    def y_copies(t):
        return [
            remote(y_send.at[t, 1], y_recv.at[t, 0], ys.at[t, 0], yr.at[t, 0], y_up),
            remote(y_send.at[t, 0], y_recv.at[t, 1], ys.at[t, 1], yr.at[t, 1], y_down),
        ]

    def z_copies(t):
        return [
            (has_above, has_below, remote(
                z_send.at[t], z_low.at[t], zs.at[t, 0], zr.at[t, 0], {"gz": gz + 1})),
            (has_below, has_above, remote(
                z_send.at[t], z_high.at[t], zs.at[t, 1], zr.at[t, 1], {"gz": gz - 1})),
        ]

    lane = lax.broadcasted_iota(jnp.int32, (cells_y, cells_z), 1)

    def pack(x, planes, acc, rows):
        for c in range(comps):
            j = c * cells_x + x
            turned = pltpu.roll(planes[c], (2 * j + 1) % cells_z, 1)
            acc = jnp.where(lane[rows] // 2 == j, turned, acc)
        return acc

    def edge_row(t, side, c, x, value):
        y_send[t, side, c * cells_x + x] = value

    def start_x(t):
        for sends, _, copy in x_copies(t):
            pl.when(sends)(copy.start)

    def start_y(t):
        for copy in y_copies(t):
            copy.start()

    def start_z(t):
        for sends, _, copy in z_copies(t):
            pl.when(sends)(copy.start)

    edge_rows = jnp.zeros((comps, cells_x, 1, cells_z), jnp.float32)
    for t in range(STEPS):
        cur[t, :, pl.ds(1, cells_x), TOP - 1:TOP, :] = edge_rows
        cur[t, :, pl.ds(1, cells_x), TOP + cells_y:TOP + cells_y + 1, :] = edge_rows

        @pl.when(gx == nx - 1)
        def _(t=t):
            cur[t, :, cells_x + 1, own, :] = jnp.zeros((comps, cells_y, cells_z), jnp.float32)

        @pl.when(gz == 0)
        def _(t=t):
            z_low[t] = jnp.zeros((cells_y, cells_z), jnp.float32)

        @pl.when(gz == nz - 1)
        def _(t=t):
            z_high[t] = jnp.zeros((cells_y, cells_z), jnp.float32)

    load_e.wait()
    load_l.wait()
    weight = blend_ref[0]

    def blended():
        mixed = (1.0 - weight) * early[...] + weight * late[...]
        return jnp.concatenate([mixed] * share, axis=2)

    feed = [remote(inflow_send, inflow_recv.at[k], fs.at[k], fr.at[k], {"gx": 0})
            for k in range(share)]

    @pl.when(feeds)
    def _():
        inflow_send[...] = blended()

    @pl.when((gx == 0) & (gz == 0))
    def _():
        inflow_recv[0] = blended()

    pl.semaphore_wait(barrier, expected)
    for k in range(share):
        @pl.when(feeds & (lax.rem(gx, share) == k))
        def _(k=k):
            feed[k].start()

    load_v.wait()

    def rows_of(x, carry):
        for c in range(comps):
            edge_row(0, 0, c, x, cur[0, c, x + 1, TOP:TOP + 1, :])
            edge_row(0, 1, c, x, cur[0, c, x + 1, TOP + cells_y - 1:TOP + cells_y, :])
        return carry

    lax.fori_loop(0, cells_x, rows_of, 0, unroll=UNROLL + 1)
    start_y(0)
    start_x(0)

    def first(x, acc):
        planes = [cur[0, c, x + 1, own, :] for c in range(comps)]
        return pack(x, planes, acc, slice(None))

    zero = jnp.zeros((cells_y, cells_z), jnp.float32)
    z_send[0] = lax.fori_loop(0, cells_x, first, zero, unroll=UNROLL + 1)
    start_z(0)

    def store(t, c, x, value):
        if t == STEPS:
            out_ref[c, x] = value
        else:
            cur[t, c, x + 1, own, :] = value

    def inner(t, x, left, right):
        q = [cur[t, c, x + 1, own, :] for c in range(comps)]
        ahead, back = [], []
        keep = jnp.float32(1.0)
        for c in range(comps):
            scaled = COURANT * q[c]
            back.append(jnp.maximum(scaled, 0.0))
            ahead.append(back[c] - scaled)
            keep = keep - jnp.abs(scaled)
        back_z = jnp.where(lane == 0, 0.0, back[2])
        ahead_z = jnp.where(lane == cells_z - 1, 0.0, ahead[2])
        for c in range(comps):
            total = (back[1] * cur[t, c, x + 1, pl.ds(TOP - 1, cells_y), :]
                     + ahead[1] * cur[t, c, x + 1, pl.ds(TOP + 1, cells_y), :])
            total += (back_z * pltpu.roll(q[c], 1, 1)
                      + ahead_z * pltpu.roll(q[c], cells_z - 1, 1))
            if left:
                total += back[0] * cur[t, c, x, own, :]
            if right:
                total += ahead[0] * cur[t, c, x + 2, own, :]
            store(t + 1, c, x, keep * q[c] + total)

    def inner_all(t):
        inner(t, 0, False, True)

        def body(x, carry):
            inner(t, x, True, True)
            return carry

        lax.fori_loop(1, cells_x - 1, body, 0, unroll=UNROLL)
        inner(t, cells_x - 1, True, False)

    middle = slice(TOP, cells_y - TOP)
    low, high = slice(0, TOP), slice(cells_y - TOP, cells_y)

    def partly(t, x, halo, acc, left=False, right=False):
        scaled = COURANT * cur[t, 2, x + 1, own, :]
        weight_z = jnp.where(
            lane == 0, jnp.maximum(scaled, 0.0),
            jnp.where(lane == cells_z - 1, jnp.maximum(-scaled, 0.0), 0.0))
        if left:
            weight_x = jnp.maximum(COURANT * cur[t, 0, x + 1, own, :], 0.0)
        if right:
            weight_x = jnp.maximum(-COURANT * cur[t, 0, x + 1, own, :], 0.0)
        planes = []
        for c in range(comps):
            j = c * cells_x + x
            value = out_ref[c, x] if t == STEPS - 1 else cur[t + 1, c, x + 1, own, :]
            value += weight_z * pltpu.roll(halo, (2 * cells_z - 2 * j) % cells_z, 1)
            if left:
                value += weight_x * cur[t, c, x, own, :]
            if right:
                value += weight_x * cur[t, c, x + 2, own, :]
            store(t + 1, c, x, value)
            planes.append(value[middle])
        return pack(x, planes, acc, middle) if t < STEPS - 1 else acc

    def edges(t, x, carry):
        weights = (jnp.maximum(COURANT * cur[t, 1, x + 1, TOP:TOP + 1, :], 0.0),
                   jnp.maximum(-COURANT * cur[t, 1, x + 1, TOP + cells_y - 1:TOP + cells_y, :], 0.0))
        for c in range(comps):
            for side, y in enumerate((0, cells_y - 1)):
                term = weights[side] * y_recv[t, side, c * cells_x + x]
                if t == STEPS - 1:
                    out_ref[c, x, y:y + 1, :] += term
                else:
                    value = cur[t + 1, c, x + 1, TOP + y:TOP + y + 1, :] + term
                    cur[t + 1, c, x + 1, TOP + y:TOP + y + 1, :] = value
                    edge_row(t + 1, side, c, x, value)
        return carry

    some = jnp.zeros((cells_y - 2 * TOP, cells_z), jnp.float32)
    few = jnp.zeros((TOP, cells_z), jnp.float32)
    for t in range(STEPS):
        inner_all(t)
        for _, recvs, copy in z_copies(t):
            pl.when(recvs)(copy.wait_recv)
        halo = jnp.where(lane % 2 == 0, z_low[t], pltpu.roll(z_high[t], cells_z - 2, 1))

        def body(x, acc, t=t, halo=halo):
            return partly(t, x, halo, acc)

        acc = lax.fori_loop(1, cells_x - 1, body, some, unroll=UNROLL)
        for _, recvs, copy in x_copies(t):
            pl.when(recvs)(copy.wait_recv)
        if t == 0:
            @pl.when(gx == 0)
            def _():
                for k in range(share):
                    @pl.when(gz * share + k != 0)
                    def _(k=k):
                        feed[k].wait_recv()
                for c in range(comps):
                    plane = inflow_recv[0, c]
                    for k in range(1, share):
                        plane = jnp.where(lane // piece == k, inflow_recv[k, c], plane)
                    for s in range(STEPS):
                        cur[s, c, 0, own, :] = plane

        acc = partly(t, 0, halo, acc, left=True)
        acc = partly(t, cells_x - 1, halo, acc, right=True)
        for copy in y_copies(t):
            copy.wait_recv()

        def rows(x, carry, t=t):
            return edges(t, x, carry)

        lax.fori_loop(0, cells_x, rows, 0, unroll=UNROLL + 1)
        if t < STEPS - 1:
            start_y(t + 1)
            start_x(t + 1)

            def ends(x, accs, t=t):
                top = [cur[t + 1, c, x + 1, pl.ds(TOP, TOP), :] for c in range(comps)]
                last = [cur[t + 1, c, x + 1, pl.ds(cells_y, TOP), :] for c in range(comps)]
                return pack(x, top, accs[0], low), pack(x, last, accs[1], high)

            top, last = lax.fori_loop(0, cells_x, ends, (few, few), unroll=UNROLL + 1)
            z_send[t + 1] = jnp.concatenate([top, acc, last], axis=0)
            start_z(t + 1)

    for t in range(STEPS):
        for sends, _, copy in x_copies(t):
            pl.when(sends)(copy.wait_send)
        for copy in y_copies(t):
            copy.wait_send()
        for sends, _, copy in z_copies(t):
            pl.when(sends)(copy.wait_send)
    for k in range(share):
        @pl.when(feeds & (lax.rem(gx, share) == k))
        def _(k=k):
            feed[k].wait_send()


def local(sizes, velocity, plane_early, plane_late, blend):
    comps, cells_x, cells_y, cells_z = velocity.shape
    nx, ny, nz = sizes
    assert nx % nz == 0 and cells_z == 128 and 2 * comps * cells_x <= cells_z
    share = nx // nz
    planes = comps * cells_x
    block = (comps, cells_y, cells_z)
    dma = pltpu.SemaphoreType.DMA
    return pl.pallas_call(
        functools.partial(kernel, sizes),
        out_shape=pltpu.VMEM(velocity.shape, velocity.dtype),
        in_specs=[pl.BlockSpec(memory_space=pl.ANY)] * 3
        + [pl.BlockSpec(memory_space=pltpu.SMEM)],
        out_specs=pl.BlockSpec(memory_space=pltpu.VMEM),
        scratch_shapes=[
            pltpu.VMEM((STEPS, comps, cells_x + 2, cells_y + 2 * TOP, cells_z), jnp.float32),
            pltpu.VMEM(plane_early.shape, jnp.float32),
            pltpu.VMEM(plane_late.shape, jnp.float32),
            pltpu.VMEM(block, jnp.float32),
            pltpu.VMEM((share,) + block, jnp.float32),
            pltpu.VMEM((STEPS, 2, planes, 1, cells_z), jnp.float32),
            pltpu.VMEM((STEPS, 2, planes, 1, cells_z), jnp.float32),
            pltpu.VMEM((STEPS, cells_y, cells_z), jnp.float32),
            pltpu.VMEM((STEPS, cells_y, cells_z), jnp.float32),
            pltpu.VMEM((STEPS, cells_y, cells_z), jnp.float32),
            dma((3,)),
            dma((STEPS, 2)), dma((STEPS, 2)),
            dma((STEPS, 2)), dma((STEPS, 2)),
            dma((STEPS, 2)), dma((STEPS, 2)),
            dma((share,)), dma((share,)),
        ],
        compiler_params=pltpu.CompilerParams(collective_id=0, has_side_effects=True),
        name="advect_substeps",
    )(velocity, plane_early, plane_late, blend)


def solution(mesh):
    sizes = tuple(mesh.shape[name] for name in ("gx", "gy", "gz"))
    return jax.shard_map(
        functools.partial(local, sizes),
        mesh=mesh,
        in_specs=(P(None, "gx", "gy", "gz"), P(None, "gy", "gx"), P(None, "gy", "gx"), P()),
        out_specs=P(None, "gx", "gy", "gz"),
        check_vma=False,
    )
```

profile of v0, /device:TPU:0, one launch (start us, length us, event | category | flops | bytes accessed | tf_op | source)
XLA Modules:
  0.0 23.4 jit_solution(3659305190805071168)
XLA Ops:
  0.7 21.8 %advect_substeps.1 = f32[3,16,32,128]{3,2,1,0:T(8,128)S(1)} custom-call(f32[3,16,32,128]{3,2,1,0:T(8,128)} %vel_hbm.1, f32[3,32,64]{2,1,0:T(8,128)} %early_hbm.1, f32[3,32,64]{2,1,0:T(8,128)} %late_hbm.1, f32[1]{0:T(128)S(6)} %copy.7.blend_ref), custom_call_target="tpu_custom_call" | custom-call | tf_op jit(solution)/shard_map/advect_substeps/pallas_call | solution.py:326
  22.5 0.9 %copy.6 = f32[3,16,32,128]{3,2,1,0:T(8,128)} copy(f32[3,16,32,128]{3,2,1,0:T(8,128)S(1)} %advect_substeps.1) | data formatting | bytes 1572864
where the time goes:
time: 23.5 us; the launch traced here: 23.4 us
  Pallas kernels  21.8 us (93%)
  local copies, waits for them, and re-layouts  0.88 us (4%)
  between operations  0.66 us (3%)
    pallas_call x1, Pallas kernels, local(): pl.pallas_call(functools.partial(kernel, sizes), out_shape=pltpu.VMEM(vel...  21.8 us
    unnamed x1, local copies, waits for them, and re-layouts  0.88 us

commit v1 on v0

v1 whole, which is shorter than its diff:
```python
import functools

import jax
import jax.numpy as jnp
from jax import lax
from jax.experimental import pallas as pl
from jax.experimental.pallas import tpu as pltpu
from jax.sharding import PartitionSpec as P

STEPS = 4
COURANT = 0.08
DEPTH = STEPS
TILE = 8
TOP = 8
GROUP = 4 * DEPTH

MESH = pl.DeviceIdType.MESH


def kernel(sizes, vel_hbm, early_hbm, late_hbm, blend_ref, out_ref,
           cur, y_halo, strip_send, strip_recv, feed_send, feed_recv, inflow, fixed,
           early, late, load_sem, ss, rs, fs, fr):
    nx, ny, nz = sizes
    comps, cells_x, cells_y, cells_z = vel_hbm.shape
    share = nx // nz
    piece = early_hbm.shape[2]
    gx, gy, gz = (lax.axis_index(name) for name in ("gx", "gy", "gz"))
    own = pl.ds(TOP, cells_y)
    first = DEPTH
    after = DEPTH + cells_x
    strips = cells_x + 2 * DEPTH
    groups = cells_z // GROUP
    rings = (cells_x + 2 * DEPTH) // groups
    half = GROUP // 2
    row_blocks = [TOP + TILE * b for b in range(cells_y // TILE)]
    low_rows, high_rows = TOP - DEPTH, TOP + cells_y - DEPTH

    load_v = pltpu.make_async_copy(
        vel_hbm, cur.at[0, :, pl.ds(first, cells_x), own, :], load_sem.at[0])
    load_e = pltpu.make_async_copy(early_hbm, early, load_sem.at[1])
    load_l = pltpu.make_async_copy(late_hbm, late, load_sem.at[2])
    load_e.start()
    load_l.start()
    load_v.start()

    has_left, has_right = gx > 0, gx < nx - 1
    always = gx >= 0
    others = {-1: has_left, 0: always, 1: has_right}

    def target(dx, dy, dz):
        where = {}
        if dx:
            where["gx"] = gx + dx
        if dy:
            where["gy"] = lax.rem(gy + dy + ny, ny)
        if dz:
            where["gz"] = 1 - gz
        return where

    needed = lambda k: (k // share == gz) | (share - gz == k)
    feeds = (gx != 0) & needed(gx)

    barrier = pltpu.get_barrier_semaphore()
    expected = jnp.int32(0)
    for dx in (0, -1, 1):
        for dy in (-1, 1, 0):
            for dz in (0, 1):
                if (dx, dy, dz) == (0, 0, 0):
                    continue

                @pl.when(others[dx])
                def _(where=target(dx, dy, dz)):
                    pl.semaphore_signal(barrier, 1, device_id=where, device_id_type=MESH)
                expected = expected + jnp.where(others[dx], 1, 0)
    for k in range(2, nx):
        for dy in (-1, 1, 0):
            @pl.when((gx == 0) & needed(k))
            def _(k=k, dy=dy):
                pl.semaphore_signal(
                    barrier, 1, device_id={"gx": k, "gy": lax.rem(gy + dy + ny, ny)},
                    device_id_type=MESH)
    expected = expected + jnp.where((gx >= 2) & feeds, 3, 0)

    count = [0]

    def message(dx, dy, dz, src, dst):
        k = count[0]
        count[0] += 1
        return others[dx], others[-dx], pltpu.make_async_remote_copy(
            src_ref=src, dst_ref=dst, send_sem=ss.at[k], recv_sem=rs.at[k],
            device_id=target(dx, dy, dz), device_id_type=MESH)

    def rows_out(dy, depth, base):
        return pl.ds(base + cells_y - depth if dy > 0 else base, depth)

    def rows_in(dy, depth, base, size):
        return pl.ds(base - depth if dy > 0 else base + size, depth)

    inside = pl.ds(first, cells_x)
    reach = DEPTH - 1
    y_messages = {}
    for dy in (1, -1):
        side = 0 if dy > 0 else 1
        into = lambda depth: rows_in(dy, depth, TILE if dy > 0 else 0, 0)
        y_messages[side] = [
            message(0, dy, 0, cur.at[0, :, inside, rows_out(dy, DEPTH, TOP), :],
                    y_halo.at[side, :, inside, into(DEPTH), :])]
        for dx in (1, -1):
            src = pl.ds(after - reach if dx > 0 else first, reach)
            dst = pl.ds(first - reach if dx > 0 else after, reach)
            y_messages[side].append(
                message(dx, dy, 0, cur.at[0, :, src, rows_out(dy, reach, TOP), :],
                        y_halo.at[side, :, dst, into(reach), :]))
        y_messages[side].append(
            message(0, dy, 1, strip_send.at[:, 0, rows_out(dy, reach, 0), :],
                    strip_recv.at[:, 0, rows_in(dy, reach, TOP, cells_y), :]))
        for dx in (1, -1):
            y_messages[side].append(
                message(dx, dy, 1, strip_send.at[:, 1, rows_out(dy, reach - 1, 0), :],
                        strip_recv.at[:, 1 if dx > 0 else 2,
                                      rows_in(dy, reach - 1, TOP, cells_y), :]))
    x_messages = [
        message(1, 0, 0, cur.at[0, :, pl.ds(after - DEPTH, DEPTH), own, :],
                cur.at[0, :, pl.ds(0, DEPTH), own, :]),
        message(-1, 0, 0, cur.at[0, :, pl.ds(first, DEPTH), own, :],
                cur.at[0, :, pl.ds(after, DEPTH), own, :])]
    z_messages = [message(0, 0, 1, strip_send.at[:, 0], strip_recv.at[:, 0, own, :])]
    for dx in (1, -1):
        z_messages.append(
            message(dx, 0, 1, strip_send.at[:, 1],
                    strip_recv.at[:, 1 if dx > 0 else 2, own, :]))

    feed_rows = {0: (pl.ds(0, cells_y), own),
                 1: (rows_out(1, reach, 0), rows_in(1, reach, TOP, cells_y)),
                 -1: (rows_out(-1, reach, 0), rows_in(-1, reach, TOP, cells_y))}

    def feed(k, dy):
        src, dst = feed_rows[dy]
        where = {"gx": 0}
        if dy:
            where["gy"] = lax.rem(gy + dy + ny, ny)
        return pltpu.make_async_remote_copy(
            src_ref=feed_send.at[:, src, :], dst_ref=feed_recv.at[k, :, dst, :],
            send_sem=fs.at[k, dy + 1], recv_sem=fr.at[k, dy + 1],
            device_id=where, device_id_type=MESH)

    def feeding(k, dy):
        if k == 0:
            return (gx == 0) & needed(0) if dy else None
        return (gx == k) & needed(k)

    def start(messages):
        for sends, _, copy in messages:
            pl.when(sends)(copy.start)

    def arrived(messages):
        for _, receives, copy in messages:
            pl.when(receives)(copy.wait_recv)

    lane = lax.broadcasted_iota(jnp.int32, (TILE, cells_z), 1)
    group = lane // GROUP
    mine = lax.rem(lane, GROUP) // half == gz
    held = ((lane >= jnp.where(gx == 0, cells_z - GROUP, cells_z))
            | (lane < jnp.where(gx == nx - 1, GROUP, 0)))
    edge = lax.rem(lane + gz * (cells_z - DEPTH), cells_z) >= cells_z - DEPTH
    up_z = jnp.where(lane == 0, 0.0, COURANT)
    down_z = jnp.where(lane == cells_z - 1, 0.0, -COURANT)

    load_e.wait()
    load_l.wait()
    weight = blend_ref[0]
    mixed = (1.0 - weight) * early[...] + weight * late[...]
    feed_send[...] = jnp.concatenate([mixed] * share, axis=2)

    load_v.wait()

    def turn(j):
        return (GROUP * j + half) % cells_z

    def pack(ring, c, rows):
        acc = None
        for j in range(groups):
            x = groups * ring + j
            p = first + x if x < cells_x + DEPTH else x - cells_x - DEPTH
            turned = pltpu.roll(cur[0, c, p, rows, :], turn(j), 1)
            acc = turned if acc is None else jnp.where(group == j, turned, acc)
        return acc

    for c in range(comps):
        for r in row_blocks:
            packed = [pack(ring, c, pl.ds(r, TILE)) for ring in range(rings - 1)]
            for ring in range(rings - 1):
                cur[0, c, strips + ring, pl.ds(r, TILE), :] = packed[ring]
            strip_send[c, 0, pl.ds(r - TOP, TILE), :] = jnp.where(
                mine, packed[0], pltpu.roll(packed[1], cells_z - half, 1))
            strip_send[c, 1, pl.ds(r - TOP, TILE), :] = jnp.where(
                group < groups // 2, packed[0], packed[-1])

    pl.semaphore_wait(barrier, expected)

    @pl.when(gy == 0)
    def _():
        start(y_messages[1])
        start(y_messages[0])

    @pl.when(gy != 0)
    def _():
        start(y_messages[0])
        start(y_messages[1])

    start(x_messages)
    start(z_messages)
    for k in range(nx):
        for dy in (0, 1, -1):
            sends = feeding(k, dy)
            if sends is not None:
                pl.when(sends)(feed(k, dy).start)

    @pl.when((gx == 0) & needed(0))
    def _():
        feed_recv[0, :, own, :] = feed_send[...]

    def advance(q, behind, ahead, inner):
        scaled = [COURANT * q[d] for d in range(3)]
        sizes_of = [jnp.abs(s) for s in scaled]
        keep = 1.0 - sizes_of[0] - sizes_of[1] - sizes_of[2]
        if inner:
            sizes_of[2] = jnp.maximum(up_z * q[2], down_z * q[2])
        positive = [q[d] > 0.0 for d in range(3)]
        result = []
        for c in range(comps):
            total = keep * q[c]
            for d in range(3):
                total += sizes_of[d] * jnp.where(positive[d], behind[d][c], ahead[d][c])
            result.append(total)
        return result

    def main(t, p, r):
        def load(dp, dr):
            return [cur[t, c, p + dp, pl.ds(r + dr, TILE), :] for c in range(comps)]

        q = load(0, 0)
        behind = [load(-1, 0), load(0, -1), [pltpu.roll(v, 1, 1) for v in q]]
        ahead = [load(1, 0), load(0, 1), [pltpu.roll(v, cells_z - 1, 1) for v in q]]
        return advance(q, behind, ahead, True)

    def merged(x, r, values):
        back = lax.rem(2 * cells_z - GROUP * lax.rem(x, groups) - half, cells_z)
        ring = strips + x // groups
        return [jnp.where(edge, pltpu.roll(cur[STEPS, c, ring, pl.ds(r, TILE), :], back, 1),
                          values[c]) for c in range(comps)]

    def planes(low, high, body, unroll):
        if low >= high:
            return
        if high - low <= unroll:
            for x in range(low, high):
                body(x)
            return

        def step(x, carry):
            body(x)
            return carry

        lax.fori_loop(low, high, step, 0, unroll=unroll)

    def block(t, low, high, unroll=2):
        def body(x):
            for r in row_blocks:
                values = main(t, x + first, r)
                if t == STEPS - 1:
                    values = merged(x, r, values)
                    for c in range(comps):
                        out_ref[c, x, pl.ds(r - TOP, TILE), :] = values[c]
                else:
                    for c in range(comps):
                        cur[t + 1, c, x + first, pl.ds(r, TILE), :] = values[c]

        planes(low, high, body, unroll)

    def window(t, low, high, side, unroll=4):
        r = high_rows if side else low_rows

        def body(x):
            values = main(t, x + first, r)
            if t == STEPS - 1:
                values = merged(x, r, values)
                for c in range(comps):
                    if side:
                        out_ref[c, x, cells_y - DEPTH:cells_y, :] = values[c][:DEPTH]
                    else:
                        out_ref[c, x, 0:DEPTH, :] = values[c][TILE - DEPTH:]
            else:
                for c in range(comps):
                    cur[t + 1, c, x + first, pl.ds(r, TILE), :] = values[c]

        planes(low, high, body, unroll)

    def around(t, r):
        def load(k, dr):
            return [cur[t, c, strips + k, pl.ds(r + dr, TILE), :] for c in range(comps)]

        ring = [load(k, 0) for k in range(rings)]
        last = t == STEPS - 1
        for k in range(rings - 1 if last else rings):
            q, before, later = ring[k], ring[k - 1], ring[(k + 1) % rings]
            behind = [
                [pltpu.roll(jnp.where(group == groups - 1, before[c], q[c]), GROUP, 1)
                 for c in range(comps)],
                load(k, -1), [pltpu.roll(v, 1, 1) for v in q]]
            ahead = [
                [pltpu.roll(jnp.where(group == 0, later[c], q[c]), cells_z - GROUP, 1)
                 for c in range(comps)],
                load(k, 1), [pltpu.roll(v, cells_z - 1, 1) for v in q]]
            values = advance(q, behind, ahead, False)
            for c in range(comps):
                value = values[c]
                if k == rings - 1:
                    value = jnp.where(held, fixed[c, pl.ds(r, TILE), :], value)
                cur[t + 1, c, strips + k, pl.ds(r, TILE), :] = value

    def assemble(r):
        rows = pl.ds(r, TILE)
        for c in range(comps):
            near = strip_recv[c, 0, rows, :]
            far = jnp.where(group < groups // 2, strip_recv[c, 2, rows, :],
                            strip_recv[c, 1, rows, :])
            theirs = [near, pltpu.roll(near, half, 1), far]
            for ring in range(rings):
                if ring < rings - 1 and r in row_blocks:
                    ours = cur[0, c, strips + ring, rows, :]
                else:
                    ours = pack(ring, c, rows)
                value = jnp.where(mine, ours, theirs[ring])
                if ring == rings - 1:
                    value = jnp.where(held, fixed[c, rows, :], value)
                cur[0, c, strips + ring, rows, :] = value

    def boundary(r, size):
        @pl.when(gx == 0)
        def _():
            for c in range(comps):
                for b in range(0, size, TILE):
                    rows = pl.ds(r + b, TILE)
                    plane = feed_recv[gz * share, c, rows, :]
                    for k in range(1, share):
                        plane = jnp.where(lane // piece == k,
                                          feed_recv[gz * share + k, c, rows, :], plane)
                    inflow[c, rows, :] = plane
                    beyond = feed_recv[share - gz, c, rows, :]
                    there = turn(groups - 1)
                    window_values = jnp.where(mine, pltpu.roll(plane, there, 1),
                                              pltpu.roll(beyond, there, 1))
                    fixed[c, rows, :] = jnp.where(group == groups - 1, window_values, 0.0)
                    for t in range(STEPS):
                        cur[t, c, first - 1, rows, :] = plane

        @pl.when(gx != 0)
        def _():
            for c in range(comps):
                for b in range(0, size, TILE):
                    fixed[c, pl.ds(r + b, TILE), :] = jnp.zeros((TILE, cells_z), jnp.float32)

        @pl.when(gx == nx - 1)
        def _():
            for c in range(comps):
                for b in range(0, size, TILE):
                    for t in range(STEPS):
                        cur[t, c, after, pl.ds(r + b, TILE), :] = jnp.zeros(
                            (TILE, cells_z), jnp.float32)

    def feed_arrived(dy):
        for k in range(nx):
            if k == 0 and dy == 0:
                continue
            pl.when((gx == 0) & needed(k))(feed(k, dy).wait_recv)

    for t in range(STEPS - 1):
        block(t, t + 1, cells_x - 1 - t)
    arrived(x_messages)
    feed_arrived(0)
    boundary(TOP, cells_y)
    for t in range(STEPS - 1):
        beyond = STEPS - 1 - t

        @pl.when(has_left)
        def _(t=t, beyond=beyond):
            block(t, -beyond, 0)

        @pl.when(has_right)
        def _(t=t, beyond=beyond):
            block(t, cells_x, cells_x + beyond)

        block(t, 0, t + 1)
        block(t, cells_x - 1 - t, cells_x)
    arrived(z_messages)

    for r in row_blocks:
        assemble(r)
    for t in range(STEPS):
        for r in row_blocks:
            around(t, r)
    block(STEPS - 1, 0, cells_x)

    def finish(side):
        r = high_rows if side else low_rows
        arrived(y_messages[side])
        feed_arrived(-1 if side else 1)
        halo = pl.ds(TOP + cells_y, DEPTH) if side else pl.ds(TOP - DEPTH, DEPTH)
        held_rows = pl.ds(0, DEPTH) if side else pl.ds(TILE - DEPTH, DEPTH)

        def copy_rows(x):
            for c in range(comps):
                cur[0, c, x + first, halo, :] = y_halo[side, c, x + first, held_rows, :]

        planes(-reach, cells_x + reach, copy_rows, 2)
        boundary(r, TILE)
        assemble(r)
        for t in range(STEPS):
            beyond = STEPS - 1 - t
            if beyond:
                @pl.when(has_left)
                def _():
                    window(t, -beyond, 0, side)

                @pl.when(has_right)
                def _():
                    window(t, cells_x, cells_x + beyond, side)
            around(t, r)
            window(t, 0, cells_x, side)

    @pl.when(gy == 0)
    def _():
        finish(1)
        finish(0)

    @pl.when(gy != 0)
    def _():
        finish(0)
        finish(1)

    for sends, _, copy in y_messages[0] + y_messages[1] + x_messages + z_messages:
        pl.when(sends)(copy.wait_send)
    for k in range(nx):
        for dy in (0, 1, -1):
            sends = feeding(k, dy)
            if sends is not None:
                pl.when(sends)(feed(k, dy).wait_send)


def local(sizes, velocity, plane_early, plane_late, blend):
    comps, cells_x, cells_y, cells_z = velocity.shape
    nx, ny, nz = sizes
    groups = cells_z // GROUP
    assert nz == 2 and ny > 2 and nx % nz == 0 and cells_z == 128
    assert cells_x == 2 * groups and 2 * DEPTH == groups and cells_y % TILE == 0
    dma = pltpu.SemaphoreType.DMA
    padded = cells_y + 2 * TOP
    planes = cells_x + 2 * DEPTH
    return pl.pallas_call(
        functools.partial(kernel, sizes),
        out_shape=pltpu.VMEM(velocity.shape, velocity.dtype),
        in_specs=[pl.BlockSpec(memory_space=pl.ANY)] * 3
        + [pl.BlockSpec(memory_space=pltpu.SMEM)],
        out_specs=pl.BlockSpec(memory_space=pltpu.VMEM),
        scratch_shapes=[
            pltpu.VMEM((STEPS + 1, comps, planes + 3, padded, cells_z), jnp.float32),
            pltpu.VMEM((2, comps, planes, TILE, cells_z), jnp.float32),
            pltpu.VMEM((comps, 2, cells_y, cells_z), jnp.float32),
            pltpu.VMEM((comps, 3, padded, cells_z), jnp.float32),
            pltpu.VMEM((comps, cells_y, cells_z), jnp.float32),
            pltpu.VMEM((nx, comps, padded, cells_z), jnp.float32),
            pltpu.VMEM((comps, padded, cells_z), jnp.float32),
            pltpu.VMEM((comps, padded, cells_z), jnp.float32),
            pltpu.VMEM(plane_early.shape, jnp.float32),
            pltpu.VMEM(plane_late.shape, jnp.float32),
            dma((3,)), dma((17,)), dma((17,)), dma((nx, 3)), dma((nx, 3)),
        ],
        compiler_params=pltpu.CompilerParams(collective_id=0, has_side_effects=True),
        name="advect_substeps",
    )(velocity, plane_early, plane_late, blend)


def solution(mesh):
    sizes = tuple(mesh.shape[name] for name in ("gx", "gy", "gz"))
    return jax.shard_map(
        functools.partial(local, sizes),
        mesh=mesh,
        in_specs=(P(None, "gx", "gy", "gz"), P(None, "gy", "gx"), P(None, "gy", "gx"), P()),
        out_specs=P(None, "gx", "gy", "gz"),
        check_vma=False,
    )
```

time: 23.5 us -> 22.7 us (0.966)
  Pallas kernels: 21.8 us -> 21 us
    pallas_call x1, Pallas kernels: 21.8 us -> 21 us  [local(): pl.pallas_call(functools.partial(kernel, sizes), out_shape=pltpu.VMEM(vel...]
where the time goes in v1:
time: 22.7 us; the launch traced here: 22.6 us
  Pallas kernels  21 us (93%)
  local copies, waits for them, and re-layouts  0.88 us (4%)
  between operations  0.66 us (3%)
    pallas_call x1, Pallas kernels, local(): pl.pallas_call(functools.partial(kernel, sizes), out_shape=pltpu.VMEM(vel...  21 us
    unnamed x1, local copies, waits for them, and re-layouts  0.88 us

profile of v1, /device:TPU:0, one launch (start us, length us, event | category | flops | bytes accessed | tf_op | source)
XLA Modules:
  0.0 22.6 jit_solution(17377038535531182477)
XLA Ops:
  0.7 21.0 %advect_substeps.1 = f32[3,16,32,128]{3,2,1,0:T(8,128)S(1)} custom-call(f32[3,16,32,128]{3,2,1,0:T(8,128)} %vel_hbm.1, f32[3,32,64]{2,1,0:T(8,128)} %early_hbm.1, f32[3,32,64]{2,1,0:T(8,128)} %late_hbm.1, f32[1]{0:T(128)S(6)} %copy.7.blend_ref), custom_call_target="tpu_custom_call" | custom-call | tf_op jit(solution)/shard_map/advect_substeps/pallas_call | solution.py:460
  21.7 0.9 %copy.6 = f32[3,16,32,128]{3,2,1,0:T(8,128)} copy(f32[3,16,32,128]{3,2,1,0:T(8,128)S(1)} %advect_substeps.1) | data formatting | bytes 1572864

commit v2 on v1

v2 whole, which is shorter than its diff:
```python
import functools

import jax
import jax.numpy as jnp
from jax import lax
from jax.experimental import pallas as pl
from jax.experimental.pallas import tpu as pltpu
from jax.sharding import PartitionSpec as P

STEPS = 4
COURANT = 0.08
DEPTH = STEPS
TILE = 8
TOP = 8
GROUP = 4 * DEPTH

MESH = pl.DeviceIdType.MESH
scope = jax.named_scope


def kernel(sizes, vel_hbm, early_hbm, late_hbm, blend_ref, out_ref,
           cur, strip_send, strip_recv, feed_send, feed_recv, inflow, fixed,
           early, late, late_sem, load_sem, ss, rs, fs, fr):
    nx, ny, nz = sizes
    comps, cells_x, cells_y, cells_z = vel_hbm.shape
    share = nx // nz
    piece = early_hbm.shape[2]
    gx, gy, gz = (lax.axis_index(name) for name in ("gx", "gy", "gz"))
    own = pl.ds(TOP, cells_y)
    first = DEPTH
    after = DEPTH + cells_x
    strips = cells_x + 2 * DEPTH
    groups = cells_z // GROUP
    rings = (cells_x + 2 * DEPTH) // groups
    half = GROUP // 2
    row_blocks = [TOP + TILE * b for b in range(cells_y // TILE)]
    low_rows, high_rows = TOP - DEPTH, TOP + cells_y - DEPTH

    load_v = pltpu.make_async_copy(
        vel_hbm, cur.at[0, :, pl.ds(first, cells_x), own, :], load_sem.at[0])
    load_e = pltpu.make_async_copy(early_hbm, early, load_sem.at[1])
    load_l = pltpu.make_async_copy(late_hbm, late, load_sem.at[2])
    load_e.start()
    load_l.start()
    load_v.start()

    has_left, has_right = gx > 0, gx < nx - 1
    always = gx >= 0
    others = {-1: has_left, 0: always, 1: has_right}
    bottom, top = gy == 0, gy == ny - 1

    def spanwise(dy):
        return lax.rem(gy + dy + ny, ny)

    def target(dx, dy, dz):
        where = {}
        if dx:
            where["gx"] = gx + dx
        if dy:
            where["gy"] = spanwise(dy)
        if dz:
            where["gz"] = 1 - gz
        return where

    def needed(k):
        return (k // share == gz) | (share - gz == k)

    feeds = (gx != 0) & needed(gx)

    barrier = pltpu.get_barrier_semaphore()
    expected = jnp.int32(0)
    late_expected = jnp.int32(0)
    late_greetings = []

    def greet(semaphore, condition, where):
        @pl.when(condition)
        def _():
            pl.semaphore_signal(semaphore, 1, device_id=where, device_id_type=MESH)

    for dy in (-1, 1, 0):
        for dx in (0, -1, 1):
            for dz in (0, 1):
                if (dx, dy, dz) == (0, 0, 0):
                    continue
                there, where = others[dx], target(dx, dy, dz)
                one = jnp.where(there, 1, 0)
                if dy == 1:
                    greet(barrier, there & ~top, where)
                    late_greetings.append((there & top, where))
                else:
                    greet(barrier, there, where)
                if dy == -1:
                    expected = expected + jnp.where(bottom, 0, one)
                    late_expected = late_expected + one
                else:
                    expected = expected + one
    for k in range(2, nx):
        takes = (gx == 0) & needed(k)
        for dy in (-1, 1, 0):
            where = {"gx": k, "gy": spanwise(dy)}
            if dy == 1:
                greet(barrier, takes & ~top, where)
                late_greetings.append((takes & top, where))
            else:
                greet(barrier, takes, where)
        greet(barrier, (gx == k) & needed(k) & bottom, {"gx": 0, "gy": spanwise(-1)})
        expected = expected + jnp.where(takes & top, 1, 0)
    gives = (gx >= 2) & feeds
    expected = expected + jnp.where(gives, jnp.where(bottom, 2, 3), 0)
    late_expected = late_expected + jnp.where(gives, 1, 0)

    count = [0]

    def message(dx, dy, dz, src, dst):
        k = count[0]
        count[0] += 1
        return others[dx], others[-dx], pltpu.make_async_remote_copy(
            src_ref=src, dst_ref=dst, send_sem=ss.at[k], recv_sem=rs.at[k],
            device_id=target(dx, dy, dz), device_id_type=MESH)

    def rows_out(dy, depth, base):
        return pl.ds(base + cells_y - depth if dy > 0 else base, depth)

    def rows_in(dy, depth):
        return pl.ds(TOP - depth if dy > 0 else TOP + cells_y, depth)

    inside = pl.ds(first, cells_x)
    reach = DEPTH - 1
    y_main, y_strips = {}, {}
    for dy in (1, -1):
        y_main[dy] = [
            message(0, dy, 0, cur.at[0, :, inside, rows_out(dy, DEPTH, TOP), :],
                    cur.at[0, :, inside, rows_in(dy, DEPTH), :])]
        for dx in (1, -1):
            src = pl.ds(after - reach if dx > 0 else first, reach)
            dst = pl.ds(first - reach if dx > 0 else after, reach)
            y_main[dy].append(
                message(dx, dy, 0, cur.at[0, :, src, rows_out(dy, reach, TOP), :],
                        cur.at[0, :, dst, rows_in(dy, reach), :]))
        y_strips[dy] = [
            message(0, dy, 1, strip_send.at[:, 0, rows_out(dy, reach, 0), :],
                    strip_recv.at[:, 0, rows_in(dy, reach), :])]
        for dx in (1, -1):
            y_strips[dy].append(
                message(dx, dy, 1, strip_send.at[:, 1, rows_out(dy, reach - 1, 0), :],
                        strip_recv.at[:, 1 if dx > 0 else 2, rows_in(dy, reach - 1), :]))
    x_messages = [
        message(1, 0, 0, cur.at[0, :, pl.ds(after - DEPTH, DEPTH), own, :],
                cur.at[0, :, pl.ds(0, DEPTH), own, :]),
        message(-1, 0, 0, cur.at[0, :, pl.ds(first, DEPTH), own, :],
                cur.at[0, :, pl.ds(after, DEPTH), own, :])]
    z_messages = [message(0, 0, 1, strip_send.at[:, 0], strip_recv.at[:, 0, own, :])]
    for dx in (1, -1):
        z_messages.append(
            message(dx, 0, 1, strip_send.at[:, 1],
                    strip_recv.at[:, 1 if dx > 0 else 2, own, :]))

    def feed(k, dy):
        where = {"gx": 0}
        if dy:
            where["gy"] = spanwise(dy)
        src = rows_out(dy, reach, 0) if dy else pl.ds(0, cells_y)
        dst = rows_in(dy, reach) if dy else own
        return pltpu.make_async_remote_copy(
            src_ref=feed_send.at[:, src, :], dst_ref=feed_recv.at[k, :, dst, :],
            send_sem=fs.at[k, dy + 1], recv_sem=fr.at[k, dy + 1],
            device_id=where, device_id_type=MESH)

    def start_feed(dy):
        for k in range(nx):
            if k or dy:
                pl.when((gx == k) & needed(k))(feed(k, dy).start)

    def feed_arrived(dy):
        for k in range(nx):
            if k or dy:
                pl.when((gx == 0) & needed(k))(feed(k, dy).wait_recv)

    def start(messages):
        for sends, _, copy in messages:
            pl.when(sends)(copy.start)

    def arrived(messages):
        for _, receives, copy in messages:
            pl.when(receives)(copy.wait_recv)

    lane = lax.broadcasted_iota(jnp.int32, (TILE, cells_z), 1)
    group = lane // GROUP
    mine = lax.rem(lane, GROUP) // half == gz
    held = ((lane >= jnp.where(gx == 0, cells_z - GROUP, cells_z))
            | (lane < jnp.where(gx == nx - 1, GROUP, 0)))
    is_first = lane >= jnp.where(gx == 0, 0, cells_z)
    is_last = lane >= jnp.where(gx == nx - 1, 0, cells_z)
    edge = lax.rem(lane + gz * (cells_z - DEPTH), cells_z) >= cells_z - DEPTH
    up_z = jnp.where(lane == 0, 0.0, COURANT)
    down_z = jnp.where(lane == cells_z - 1, 0.0, -COURANT)

    with scope("load_el"):
        load_e.wait()
        load_l.wait()
    weight = blend_ref[0]
    mixed = (1.0 - weight) * early[...] + weight * late[...]
    feed_send[...] = jnp.concatenate([mixed] * share, axis=2)

    with scope("load_v"):
        load_v.wait()
    with scope("barrier"):
        pl.semaphore_wait(barrier, expected)
    with scope("send"):
        start(y_main[1])
        pl.when(~bottom)(lambda: start(y_main[-1]))
        start_feed(0)
        start(x_messages)
        for condition, where in late_greetings:
            greet(late_sem, condition, where)

    def turn(j):
        return (GROUP * j + half) % cells_z

    def pack(ring, c, rows):
        acc = None
        for j in range(groups):
            x = groups * ring + j
            p = first + x if x < cells_x + DEPTH else x - cells_x - DEPTH
            turned = pltpu.roll(cur[0, c, p, rows, :], turn(j), 1)
            acc = turned if acc is None else jnp.where(group == j, turned, acc)
        return acc

    with scope("pack"):
        for r in row_blocks:
            for c in range(comps):
                packed = [pack(ring, c, pl.ds(r, TILE)) for ring in range(rings - 1)]
                for ring in range(rings - 1):
                    cur[0, c, strips + ring, pl.ds(r, TILE), :] = packed[ring]
                strip_send[c, 0, pl.ds(r - TOP, TILE), :] = jnp.where(
                    mine, packed[0], pltpu.roll(packed[1], cells_z - half, 1))
                strip_send[c, 1, pl.ds(r - TOP, TILE), :] = jnp.where(
                    group < groups // 2, packed[0], packed[-1])

    with scope("send2"):
        start(y_strips[1])
        start(z_messages)
        start_feed(1)

        @pl.when(~bottom)
        def _():
            start(y_strips[-1])
            start_feed(-1)

    @pl.when((gx == 0) & needed(0))
    def _():
        feed_recv[0, :, own, :] = feed_send[...]

    def advance(q, behind, ahead, inner):
        scaled = [COURANT * q[d] for d in range(3)]
        weights = [jnp.abs(s) for s in scaled]
        keep = 1.0 - weights[0] - weights[1] - weights[2]
        if inner:
            weights[2] = jnp.maximum(up_z * q[2], down_z * q[2])
        positive = [q[d] > 0.0 for d in range(3)]
        result = []
        for c in range(comps):
            total = keep * q[c]
            for d in range(3):
                total += weights[d] * jnp.where(positive[d], behind[d][c], ahead[d][c])
            result.append(total)
        return result

    def shifted(t, p, r, dr, q):
        rows = r + dr
        if t == 0 and r in row_blocks and (rows < TOP or rows + TILE > TOP + cells_y):
            return [pltpu.roll(v, 1 if dr < 0 else TILE - 1, 0) for v in q]
        return [cur[t, c, p, pl.ds(rows, TILE), :] for c in range(comps)]

    def main(t, p, r):
        q, left, right = ([cur[t, c, p + dp, pl.ds(r, TILE), :] for c in range(comps)]
                          for dp in (0, -1, 1))
        behind = [left, shifted(t, p, r, -1, q), [pltpu.roll(v, 1, 1) for v in q]]
        ahead = [right, shifted(t, p, r, 1, q), [pltpu.roll(v, cells_z - 1, 1) for v in q]]
        return advance(q, behind, ahead, True)

    def merged(x, r, values):
        back = lax.rem(2 * cells_z - GROUP * lax.rem(x, groups) - half, cells_z)
        ring = strips + x // groups
        return [jnp.where(edge, pltpu.roll(cur[STEPS, c, ring, pl.ds(r, TILE), :], back, 1),
                          values[c]) for c in range(comps)]

    def plane(t, x, rows):
        for r in rows:
            values = main(t, x + first, r)
            if t < STEPS - 1:
                if isinstance(x, int) and x == -1:
                    values = [jnp.where(is_first, inflow[c, pl.ds(r, TILE), :], values[c])
                              for c in range(comps)]
                if isinstance(x, int) and x == cells_x:
                    values = [jnp.where(is_last, 0.0, v) for v in values]
                for c in range(comps):
                    cur[t + 1, c, x + first, pl.ds(r, TILE), :] = values[c]
                continue
            values = merged(x, r, values)
            for c in range(comps):
                if r == low_rows:
                    out_ref[c, x, 0:DEPTH, :] = values[c][TILE - DEPTH:]
                elif r == high_rows:
                    out_ref[c, x, cells_y - DEPTH:cells_y, :] = values[c][:DEPTH]
                else:
                    out_ref[c, x, pl.ds(r - TOP, TILE), :] = values[c]

    def planes(t, low, high, rows, unroll=None):
        cuts = sorted({low, high} | {k for k in (-1, 0, cells_x, cells_x + 1)
                                     if low < k < high})
        for begin, end in zip(cuts[:-1], cuts[1:]):
            if end - begin == 1:
                plane(t, begin, rows)
                continue

            def step(x, carry):
                plane(t, x, rows)
                return carry

            lax.fori_loop(begin, end, step, 0, unroll=unroll or end - begin)

    def around(t, r):
        ring = [[cur[t, c, strips + k, pl.ds(r, TILE), :] for c in range(comps)]
                for k in range(rings)]
        last = t == STEPS - 1

        def load(k, dr):
            return [cur[t, c, strips + k, pl.ds(r + dr, TILE), :] for c in range(comps)]

        for k in range(rings - 1 if last else rings):
            q, before, later = ring[k], ring[k - 1], ring[(k + 1) % rings]
            behind = [
                [pltpu.roll(jnp.where(group == groups - 1, before[c], q[c]), GROUP, 1)
                 for c in range(comps)],
                load(k, -1), [pltpu.roll(v, 1, 1) for v in q]]
            ahead = [
                [pltpu.roll(jnp.where(group == 0, later[c], q[c]), cells_z - GROUP, 1)
                 for c in range(comps)],
                load(k, 1), [pltpu.roll(v, cells_z - 1, 1) for v in q]]
            values = advance(q, behind, ahead, False)
            for c in range(comps):
                value = values[c]
                if k == rings - 1:
                    value = jnp.where(held, fixed[c, pl.ds(r, TILE), :], value)
                cur[t + 1, c, strips + k, pl.ds(r, TILE), :] = value

    def assemble(r):
        rows = pl.ds(r, TILE)
        for c in range(comps):
            near = strip_recv[c, 0, rows, :]
            far = jnp.where(group < groups // 2, strip_recv[c, 2, rows, :],
                            strip_recv[c, 1, rows, :])
            theirs = [near, pltpu.roll(near, half, 1), far]
            for ring in range(rings):
                if ring < rings - 1 and r in row_blocks:
                    ours = cur[0, c, strips + ring, rows, :]
                else:
                    ours = pack(ring, c, rows)
                value = jnp.where(mine, ours, theirs[ring])
                if ring == rings - 1:
                    value = jnp.where(held, fixed[c, rows, :], value)
                cur[0, c, strips + ring, rows, :] = value

    def ghosts(r):
        rows = pl.ds(r, TILE)
        for c in range(comps):
            values = feed_recv[gz * share, c, rows, :]
            for k in range(1, share):
                values = jnp.where(lane // piece == k,
                                   feed_recv[gz * share + k, c, rows, :], values)
            inflow[c, rows, :] = values
            beyond = feed_recv[share - gz, c, rows, :]
            there = turn(groups - 1)
            there_values = jnp.where(mine, pltpu.roll(values, there, 1),
                                     pltpu.roll(beyond, there, 1))
            fixed[c, rows, :] = jnp.where(is_first & (group == groups - 1), there_values, 0.0)
            cur[0, c, first - 1, rows, :] = jnp.where(
                is_first, values, cur[0, c, first - 1, rows, :])
            cur[0, c, after, rows, :] = jnp.where(is_last, 0.0, cur[0, c, after, rows, :])

    for t in range(STEPS - 1):
        with scope("A1_%d" % t):
            planes(t, t + 1, cells_x - 1 - t, row_blocks)

    @pl.when(bottom)
    def _():
        with scope("late"):
            pl.semaphore_wait(late_sem, late_expected)
        start(y_main[-1])
        start(y_strips[-1])
        start_feed(-1)

    with scope("x_wait"):
        arrived(x_messages)
    with scope("feed_wait"):
        feed_arrived(0)
    with scope("A2"):
        for r in row_blocks:
            ghosts(r)
        for t in range(STEPS - 1):
            beyond = STEPS - 1 - t
            planes(t, -beyond, t + 1, row_blocks)
            planes(t, cells_x - 1 - t, cells_x + beyond, row_blocks)
    with scope("z_wait"):
        arrived(z_messages)
    with scope("around"):
        for r in row_blocks:
            assemble(r)
        for t in range(STEPS):
            for r in row_blocks:
                around(t, r)
    with scope("final"):
        planes(STEPS - 1, 0, cells_x, row_blocks)

    def finish(dy):
        r = low_rows if dy > 0 else high_rows
        with scope("y_wait%d" % dy):
            arrived(y_main[dy])
            arrived(y_strips[dy])
            feed_arrived(dy)
        with scope("win%d" % dy):
            ghosts(r)
            assemble(r)
            for t in range(STEPS):
                beyond = STEPS - 1 - t
                around(t, r)
                planes(t, -beyond, cells_x + beyond, [r])

    @pl.when(bottom)
    def _():
        finish(-1)
        finish(1)

    @pl.when(~bottom)
    def _():
        finish(1)
        finish(-1)

    with scope("drain"):
        for dy in (1, -1):
            for sends, _, copy in y_main[dy] + y_strips[dy]:
                pl.when(sends)(copy.wait_send)
        for sends, _, copy in x_messages + z_messages:
            pl.when(sends)(copy.wait_send)
        for k in range(nx):
            for dy in (0, 1, -1):
                if k or dy:
                    pl.when((gx == k) & needed(k))(feed(k, dy).wait_send)


def local(sizes, velocity, plane_early, plane_late, blend):
    comps, cells_x, cells_y, cells_z = velocity.shape
    nx, ny, nz = sizes
    groups = cells_z // GROUP
    assert nz == 2 and ny > 2 and nx % nz == 0 and cells_z == 128
    assert cells_x == 2 * groups and 2 * DEPTH == groups and cells_y % TILE == 0
    dma = pltpu.SemaphoreType.DMA
    padded = cells_y + 2 * TOP
    planes = cells_x + 2 * DEPTH
    return pl.pallas_call(
        functools.partial(kernel, sizes),
        out_shape=pltpu.VMEM(velocity.shape, velocity.dtype),
        in_specs=[pl.BlockSpec(memory_space=pl.ANY)] * 3
        + [pl.BlockSpec(memory_space=pltpu.SMEM)],
        out_specs=pl.BlockSpec(memory_space=pltpu.VMEM),
        scratch_shapes=[
            pltpu.VMEM((STEPS + 1, comps, planes + 3, padded, cells_z), jnp.float32),
            pltpu.VMEM((comps, 2, cells_y, cells_z), jnp.float32),
            pltpu.VMEM((comps, 3, padded, cells_z), jnp.float32),
            pltpu.VMEM((comps, cells_y, cells_z), jnp.float32),
            pltpu.VMEM((nx, comps, padded, cells_z), jnp.float32),
            pltpu.VMEM((comps, padded, cells_z), jnp.float32),
            pltpu.VMEM((comps, padded, cells_z), jnp.float32),
            pltpu.VMEM(plane_early.shape, jnp.float32),
            pltpu.VMEM(plane_late.shape, jnp.float32),
            pltpu.SemaphoreType.REGULAR,
            dma((3,)), dma((17,)), dma((17,)), dma((nx, 3)), dma((nx, 3)),
        ],
        compiler_params=pltpu.CompilerParams(collective_id=0, has_side_effects=True),
        name="advect_substeps",
    )(velocity, plane_early, plane_late, blend)


def solution(mesh):
    sizes = tuple(mesh.shape[name] for name in ("gx", "gy", "gz"))
    return jax.shard_map(
        functools.partial(local, sizes),
        mesh=mesh,
        in_specs=(P(None, "gx", "gy", "gz"), P(None, "gy", "gx"), P(None, "gy", "gx"), P()),
        out_specs=P(None, "gx", "gy", "gz"),
        check_vma=False,
    )
```

time: 22.7 us -> 17.4 us (0.77)
  Pallas kernels: 21 us -> 15.7 us
    pallas_call x1, Pallas kernels: 21 us -> 15.7 us  [local(): pl.pallas_call(functools.partial(kernel, sizes), out_shape=pltpu.VMEM(vel...]
where the time goes in v2:
time: 17.4 us; the launch traced here: 17.3 us
  Pallas kernels  15.7 us (90%)
  local copies, waits for them, and re-layouts  0.88 us (5%)
  between operations  0.66 us (4%)
    pallas_call x1, Pallas kernels, local(): pl.pallas_call(functools.partial(kernel, sizes), out_shape=pltpu.VMEM(vel...  15.7 us
    unnamed x1, local copies, waits for them, and re-layouts  0.88 us

profile of v2, /device:TPU:0, one launch (start us, length us, event | category | flops | bytes accessed | tf_op | source)
XLA Modules:
  0.0 17.3 jit_solution(7168117771871133785)
XLA Ops:
  0.7 15.7 %advect_substeps.1 = f32[3,16,32,128]{3,2,1,0:T(8,128)S(1)} custom-call(f32[3,16,32,128]{3,2,1,0:T(8,128)} %vel_hbm.1, f32[3,32,64]{2,1,0:T(8,128)} %early_hbm.1, f32[3,32,64]{2,1,0:T(8,128)} %late_hbm.1, f32[1]{0:T(128)S(6)} %copy.7.blend_ref), custom_call_target="tpu_custom_call" | custom-call | tf_op jit(solution)/shard_map/advect_substeps/pallas_call | solution.py:461
  16.4 0.9 %copy.6 = f32[3,16,32,128]{3,2,1,0:T(8,128)} copy(f32[3,16,32,128]{3,2,1,0:T(8,128)S(1)} %advect_substeps.1) | data formatting | bytes 1572864

commit v3 on v2

--- a/solution.py
+++ b/solution.py
@@ -20,7 +20,7 @@
 
 def kernel(sizes, vel_hbm, early_hbm, late_hbm, blend_ref, out_ref,
            cur, strip_send, strip_recv, feed_send, feed_recv, inflow, fixed,
-           early, late, late_sem, load_sem, ss, rs, fs, fr):
+           early, late, tally, late_sem, load_sem, send_sem, recv_sem):
     nx, ny, nz = sizes
     comps, cells_x, cells_y, cells_z = vel_hbm.shape
     share = nx // nz
@@ -67,56 +67,89 @@
 
     feeds = (gx != 0) & needed(gx)
 
+    def gain(dx, dy, dz):
+        step = lax.div(gx + dx + 2, 2) - lax.div(gx + 2, 2)
+        if dy:
+            step = step + spanwise(dy) - gy
+        return step + 1 - 2 * gz if dz else step
+
     barrier = pltpu.get_barrier_semaphore()
+    NEAR, FAR = 0, 1
     expected = jnp.int32(0)
-    late_expected = jnp.int32(0)
+    late_expected = [jnp.int32(0), jnp.int32(0)]
     late_greetings = []
+    soon, far = {}, {}
 
     def greet(semaphore, condition, where):
         @pl.when(condition)
         def _():
             pl.semaphore_signal(semaphore, 1, device_id=where, device_id_type=MESH)
 
+    def await_greetings(semaphore, number):
+        @pl.when(number > 0)
+        def _():
+            pl.semaphore_wait(semaphore, number)
+
     for dy in (-1, 1, 0):
         for dx in (0, -1, 1):
             for dz in (0, 1):
-                if (dx, dy, dz) == (0, 0, 0):
+                place = (dx, dy, dz)
+                if place == (0, 0, 0):
                     continue
-                there, where = others[dx], target(dx, dy, dz)
-                one = jnp.where(there, 1, 0)
+                there, where, later = others[dx], target(*place), gain(*place)
+                greet(barrier, there & (later >= 0), where)
+                beyond = top if dy == 1 else gy < 0
+                late_greetings.append((NEAR, there & (later < 0) & ~beyond, where))
                 if dy == 1:
-                    greet(barrier, there & ~top, where)
-                    late_greetings.append((there & top, where))
-                else:
-                    greet(barrier, there, where)
-                if dy == -1:
-                    expected = expected + jnp.where(bottom, 0, one)
-                    late_expected = late_expected + one
-                else:
-                    expected = expected + one
+                    late_greetings.append((FAR, there & (later < 0) & beyond, where))
+                soon[place] = later <= 0
+                far[place] = (later > 0) & bottom if dy == -1 else gy < 0
+                expected = expected + jnp.where(there & soon[place], 1, 0)
+                late_expected[NEAR] = late_expected[NEAR] + jnp.where(
+                    there & ~soon[place] & ~far[place], 1, 0)
+                late_expected[FAR] = late_expected[FAR] + jnp.where(there & far[place], 1, 0)
     for k in range(2, nx):
         takes = (gx == 0) & needed(k)
         for dy in (-1, 1, 0):
             where = {"gx": k, "gy": spanwise(dy)}
             if dy == 1:
                 greet(barrier, takes & ~top, where)
-                late_greetings.append((takes & top, where))
+                late_greetings.append((FAR, takes & top, where))
             else:
                 greet(barrier, takes, where)
         greet(barrier, (gx == k) & needed(k) & bottom, {"gx": 0, "gy": spanwise(-1)})
         expected = expected + jnp.where(takes & top, 1, 0)
     gives = (gx >= 2) & feeds
     expected = expected + jnp.where(gives, jnp.where(bottom, 2, 3), 0)
-    late_expected = late_expected + jnp.where(gives, 1, 0)
-
-    count = [0]
-
-    def message(dx, dy, dz, src, dst):
-        k = count[0]
-        count[0] += 1
-        return others[dx], others[-dx], pltpu.make_async_remote_copy(
-            src_ref=src, dst_ref=dst, send_sem=ss.at[k], recv_sem=rs.at[k],
+    late_expected[FAR] = late_expected[FAR] + jnp.where(gives & bottom, 1, 0)
+
+    Y_UP, Y_DOWN, X, Z, FEED = range(5)
+    y_group = {1: Y_UP, -1: Y_DOWN}
+    volume = {}
+
+    def rows_of(ref):
+        rows = 1
+        for extent in ref.shape[:-1]:
+            rows *= extent
+        return rows
+
+    def message(group, dx, dy, dz, src, dst):
+        volume[group, dx] = volume.get((group, dx), 0) + rows_of(src)
+        return (dx, dy, dz), pltpu.make_async_remote_copy(
+            src_ref=src, dst_ref=dst, send_sem=send_sem.at[0], recv_sem=recv_sem.at[group],
             device_id=target(dx, dy, dz), device_id_type=MESH)
+
+    def settle(semaphore, rows):
+        part = tally.at[pl.ds(0, rows)]
+        pltpu.make_async_copy(part, part, semaphore).wait()
+
+    at_left, at_right = gx == 0, gx == nx - 1
+
+    def settle_by_place(semaphore, from_left, middle, from_right, extra_left=0):
+        pl.when(at_left)(lambda: settle(semaphore, middle + from_right + extra_left))
+        pl.when(at_right)(lambda: settle(semaphore, middle + from_left))
+        pl.when(~at_left & ~at_right)(
+            lambda: settle(semaphore, middle + from_left + from_right))
 
     def rows_out(dy, depth, base):
         return pl.ds(base + cells_y - depth if dy > 0 else base, depth)
@@ -128,32 +161,37 @@
     reach = DEPTH - 1
     y_main, y_strips = {}, {}
     for dy in (1, -1):
-        y_main[dy] = [
-            message(0, dy, 0, cur.at[0, :, inside, rows_out(dy, DEPTH, TOP), :],
-                    cur.at[0, :, inside, rows_in(dy, DEPTH), :])]
+        g = y_group[dy]
+        y_main[dy] = []
         for dx in (1, -1):
-            src = pl.ds(after - reach if dx > 0 else first, reach)
-            dst = pl.ds(first - reach if dx > 0 else after, reach)
-            y_main[dy].append(
-                message(dx, dy, 0, cur.at[0, :, src, rows_out(dy, reach, TOP), :],
-                        cur.at[0, :, dst, rows_in(dy, reach), :]))
+            for d in range(1, DEPTH):
+                src = after - d if dx > 0 else first + d - 1
+                dst = first - d if dx > 0 else after + d - 1
+                y_main[dy].append(
+                    message(g, dx, dy, 0, cur.at[0, :, src, rows_out(dy, DEPTH - d, TOP), :],
+                            cur.at[0, :, dst, rows_in(dy, DEPTH - d), :]))
+        y_main[dy].append(
+            message(g, 0, dy, 0, cur.at[0, :, inside, rows_out(dy, DEPTH, TOP), :],
+                    cur.at[0, :, inside, rows_in(dy, DEPTH), :]))
         y_strips[dy] = [
-            message(0, dy, 1, strip_send.at[:, 0, rows_out(dy, reach, 0), :],
-                    strip_recv.at[:, 0, rows_in(dy, reach), :])]
+            message(g, 0, dy, 1, strip_send.at[pl.ds(0, comps), rows_out(dy, reach, 0), :],
+                    strip_recv.at[pl.ds(0, comps), rows_in(dy, reach), :])]
         for dx in (1, -1):
+            slot = comps if dx > 0 else comps + 1
             y_strips[dy].append(
-                message(dx, dy, 1, strip_send.at[:, 1, rows_out(dy, reach - 1, 0), :],
-                        strip_recv.at[:, 1 if dx > 0 else 2, rows_in(dy, reach - 1), :]))
+                message(g, dx, dy, 1, strip_send.at[slot, rows_out(dy, reach - 1, 0), :],
+                        strip_recv.at[slot, rows_in(dy, reach - 1), :]))
     x_messages = [
-        message(1, 0, 0, cur.at[0, :, pl.ds(after - DEPTH, DEPTH), own, :],
+        message(X, 1, 0, 0, cur.at[0, :, pl.ds(after - DEPTH, DEPTH), own, :],
                 cur.at[0, :, pl.ds(0, DEPTH), own, :]),
-        message(-1, 0, 0, cur.at[0, :, pl.ds(first, DEPTH), own, :],
+        message(X, -1, 0, 0, cur.at[0, :, pl.ds(first, DEPTH), own, :],
                 cur.at[0, :, pl.ds(after, DEPTH), own, :])]
-    z_messages = [message(0, 0, 1, strip_send.at[:, 0], strip_recv.at[:, 0, own, :])]
+    z_messages = [message(Z, 0, 0, 1, strip_send.at[pl.ds(0, comps)],
+                          strip_recv.at[pl.ds(0, comps), own, :])]
     for dx in (1, -1):
+        slot = comps if dx > 0 else comps + 1
         z_messages.append(
-            message(dx, 0, 1, strip_send.at[:, 1],
-                    strip_recv.at[:, 1 if dx > 0 else 2, own, :]))
+            message(Z, dx, 0, 1, strip_send.at[slot], strip_recv.at[slot, own, :]))
 
     def feed(k, dy):
         where = {"gx": 0}
@@ -163,26 +201,36 @@
         dst = rows_in(dy, reach) if dy else own
         return pltpu.make_async_remote_copy(
             src_ref=feed_send.at[:, src, :], dst_ref=feed_recv.at[k, :, dst, :],
-            send_sem=fs.at[k, dy + 1], recv_sem=fr.at[k, dy + 1],
+            send_sem=send_sem.at[1], recv_sem=recv_sem.at[y_group[dy] if dy else FEED],
             device_id=where, device_id_type=MESH)
 
-    def start_feed(dy):
-        for k in range(nx):
+    def start_feed(dy, condition, ks=None):
+        for k in ks or range(nx):
             if k or dy:
-                pl.when((gx == k) & needed(k))(feed(k, dy).start)
-
-    def feed_arrived(dy):
-        for k in range(nx):
-            if k or dy:
-                pl.when((gx == 0) & needed(k))(feed(k, dy).wait_recv)
-
-    def start(messages):
-        for sends, _, copy in messages:
-            pl.when(sends)(copy.start)
-
-    def arrived(messages):
-        for _, receives, copy in messages:
-            pl.when(receives)(copy.wait_recv)
+                pl.when((gx == k) & needed(k) & condition)(feed(k, dy).start)
+
+    def pieces(z, dy):
+        return [k for k in range(nx)
+                if (k or dy) and (k // share == z or share - z == k)]
+
+    def start(messages, phase, condition=None):
+        for place, copy in messages:
+            late = ~soon[place] & ~far[place]
+            when = others[place[0]] & (soon[place], late, far[place])[phase]
+            pl.when(when if condition is None else when & condition)(copy.start)
+
+    def group_arrived(g, extra_left=0):
+        settle_by_place(recv_sem.at[g], volume.get((g, 1), 0), volume.get((g, 0), 0),
+                        volume.get((g, -1), 0), extra_left)
+
+    def y_arrived(dy):
+        assert len(pieces(0, dy)) == len(pieces(1, dy))
+        group_arrived(y_group[dy], len(pieces(0, dy)) * comps * reach)
+
+    def feed_arrived():
+        for z in range(nz):
+            pl.when(at_left & (gz == z))(
+                lambda z=z: settle(recv_sem.at[FEED], len(pieces(z, 0)) * comps * cells_y))
 
     lane = lax.broadcasted_iota(jnp.int32, (TILE, cells_z), 1)
     group = lane // GROUP
@@ -204,15 +252,7 @@
 
     with scope("load_v"):
         load_v.wait()
-    with scope("barrier"):
-        pl.semaphore_wait(barrier, expected)
-    with scope("send"):
-        start(y_main[1])
-        pl.when(~bottom)(lambda: start(y_main[-1]))
-        start_feed(0)
-        start(x_messages)
-        for condition, where in late_greetings:
-            greet(late_sem, condition, where)
+    swap = half + gz * (cells_z - GROUP)
 
     def turn(j):
         return (GROUP * j + half) % cells_z
@@ -226,26 +266,43 @@
             acc = turned if acc is None else jnp.where(group == j, turned, acc)
         return acc
 
-    with scope("pack"):
-        for r in row_blocks:
+    def pack_rows(blocks):
+        for r in blocks:
+            outer = [[], []]
             for c in range(comps):
                 packed = [pack(ring, c, pl.ds(r, TILE)) for ring in range(rings - 1)]
                 for ring in range(rings - 1):
                     cur[0, c, strips + ring, pl.ds(r, TILE), :] = packed[ring]
-                strip_send[c, 0, pl.ds(r - TOP, TILE), :] = jnp.where(
+                strip_send[c, pl.ds(r - TOP, TILE), :] = jnp.where(
                     mine, packed[0], pltpu.roll(packed[1], cells_z - half, 1))
-                strip_send[c, 1, pl.ds(r - TOP, TILE), :] = jnp.where(
-                    group < groups // 2, packed[0], packed[-1])
-
+                outer[0].append(packed[-1])
+                outer[1].append(packed[0])
+            for d in range(2):
+                side = group >= groups // 2 if d == 0 else group < groups // 2
+                strip_send[comps + d, pl.ds(r - TOP, TILE), :] = jnp.where(
+                    side, jnp.where(mine, outer[d][0], pltpu.roll(outer[d][1], swap, 1)),
+                    pltpu.roll(outer[d][2], cells_z // 2, 1))
+
+    with scope("pack"):
+        pack_rows([row_blocks[0], row_blocks[-1]])
+    with scope("barrier"):
+        await_greetings(barrier, expected)
+    with scope("send"):
+        start(y_strips[1], 0)
+        start_feed(1, always, range(2, nx))
+        start_feed(1, top, range(2))
+        start(y_main[1], 0)
+        start(y_strips[-1], 0)
+        start_feed(-1, ~bottom)
+        start(y_main[-1], 0)
+        start_feed(0, always)
+        start(x_messages, 0)
+        for which, condition, where in late_greetings:
+            greet(late_sem.at[which], condition, where)
+    with scope("pack2"):
+        pack_rows(row_blocks[1:-1])
     with scope("send2"):
-        start(y_strips[1])
-        start(z_messages)
-        start_feed(1)
-
-        @pl.when(~bottom)
-        def _():
-            start(y_strips[-1])
-            start_feed(-1)
+        start(z_messages, 0)
 
     @pl.when((gx == 0) & needed(0))
     def _():
@@ -347,11 +404,14 @@
 
     def assemble(r):
         rows = pl.ds(r, TILE)
+        low = group < groups // 2
+        before, later = strip_recv[comps, rows, :], strip_recv[comps + 1, rows, :]
+        mixed_far = jnp.where(low, later, before)
+        far = [mixed_far, pltpu.roll(mixed_far, swap, 1),
+               pltpu.roll(jnp.where(low, before, later), cells_z // 2, 1)]
         for c in range(comps):
-            near = strip_recv[c, 0, rows, :]
-            far = jnp.where(group < groups // 2, strip_recv[c, 2, rows, :],
-                            strip_recv[c, 1, rows, :])
-            theirs = [near, pltpu.roll(near, half, 1), far]
+            near = strip_recv[c, rows, :]
+            theirs = [near, pltpu.roll(near, half, 1), far[c]]
             for ring in range(rings):
                 if ring < rings - 1 and r in row_blocks:
                     ours = cur[0, c, strips + ring, rows, :]
@@ -383,18 +443,25 @@
         with scope("A1_%d" % t):
             planes(t, t + 1, cells_x - 1 - t, row_blocks)
 
+    with scope("late"):
+        await_greetings(late_sem.at[NEAR], late_expected[NEAR])
+        start(y_strips[1], 1)
+        start_feed(1, ~top, range(2))
+        for messages in (y_main[1], y_strips[-1], y_main[-1], z_messages, x_messages):
+            start(messages, 1)
+
     @pl.when(bottom)
     def _():
-        with scope("late"):
-            pl.semaphore_wait(late_sem, late_expected)
-        start(y_main[-1])
-        start(y_strips[-1])
-        start_feed(-1)
+        with scope("far"):
+            await_greetings(late_sem.at[FAR], late_expected[FAR])
+            start(y_strips[-1], 2)
+            start_feed(-1, always)
+            start(y_main[-1], 2)
 
     with scope("x_wait"):
-        arrived(x_messages)
+        group_arrived(X)
     with scope("feed_wait"):
-        feed_arrived(0)
+        feed_arrived()
     with scope("A2"):
         for r in row_blocks:
             ghosts(r)
@@ -403,7 +470,7 @@
             planes(t, -beyond, t + 1, row_blocks)
             planes(t, cells_x - 1 - t, cells_x + beyond, row_blocks)
     with scope("z_wait"):
-        arrived(z_messages)
+        group_arrived(Z)
     with scope("around"):
         for r in row_blocks:
             assemble(r)
@@ -416,9 +483,7 @@
     def finish(dy):
         r = low_rows if dy > 0 else high_rows
         with scope("y_wait%d" % dy):
-            arrived(y_main[dy])
-            arrived(y_strips[dy])
-            feed_arrived(dy)
+            y_arrived(dy)
         with scope("win%d" % dy):
             ghosts(r)
             assemble(r)
@@ -438,15 +503,12 @@
         finish(-1)
 
     with scope("drain"):
-        for dy in (1, -1):
-            for sends, _, copy in y_main[dy] + y_strips[dy]:
-                pl.when(sends)(copy.wait_send)
-        for sends, _, copy in x_messages + z_messages:
-            pl.when(sends)(copy.wait_send)
-        for k in range(nx):
-            for dy in (0, 1, -1):
-                if k or dy:
-                    pl.when((gx == k) & needed(k))(feed(k, dy).wait_send)
+        total = {dx: sum(rows for (_, d), rows in volume.items() if d == dx)
+                 for dx in (-1, 0, 1)}
+        settle_by_place(send_sem.at[0], total[-1], total[0], total[1])
+        fed = comps * (cells_y + 2 * reach)
+        pl.when(feeds)(lambda: settle(send_sem.at[1], fed))
+        pl.when(at_left & needed(0))(lambda: settle(send_sem.at[1], 2 * comps * reach))
 
 
 def local(sizes, velocity, plane_early, plane_late, blend):
@@ -466,16 +528,16 @@
         out_specs=pl.BlockSpec(memory_space=pltpu.VMEM),
         scratch_shapes=[
             pltpu.VMEM((STEPS + 1, comps, planes + 3, padded, cells_z), jnp.float32),
-            pltpu.VMEM((comps, 2, cells_y, cells_z), jnp.float32),
-            pltpu.VMEM((comps, 3, padded, cells_z), jnp.float32),
+            pltpu.VMEM((comps + 2, cells_y, cells_z), jnp.float32),
+            pltpu.VMEM((comps + 2, padded, cells_z), jnp.float32),
             pltpu.VMEM((comps, cells_y, cells_z), jnp.float32),
             pltpu.VMEM((nx, comps, padded, cells_z), jnp.float32),
             pltpu.VMEM((comps, padded, cells_z), jnp.float32),
             pltpu.VMEM((comps, padded, cells_z), jnp.float32),
             pltpu.VMEM(plane_early.shape, jnp.float32),
             pltpu.VMEM(plane_late.shape, jnp.float32),
-            pltpu.SemaphoreType.REGULAR,
-            dma((3,)), dma((17,)), dma((17,)), dma((nx, 3)), dma((nx, 3)),
+            pltpu.VMEM((2 * comps * planes * padded, cells_z), jnp.float32),
+            pltpu.SemaphoreType.REGULAR((2,)), dma((3,)), dma((2,)), dma((5,)),
         ],
         compiler_params=pltpu.CompilerParams(collective_id=0, has_side_effects=True),
         name="advect_substeps",

time: 17.4 us -> 15.3 us (0.88)
  the two profiles are of different devices: /device:TPU:0 before, /device:TPU:25 now
where the time goes in v3:
time: 15.3 us; the launch traced here: 15.1 us
  Pallas kernels  13.6 us (89%)
  local copies, waits for them, and re-layouts  0.88 us (6%)
  between operations  0.66 us (4%)
    pallas_call x1, Pallas kernels, local(): pl.pallas_call(functools.partial(kernel, sizes), out_shape=pltpu.VMEM(vel...  13.6 us
    unnamed x1, local copies, waits for them, and re-layouts  0.88 us

profile of v3, /device:TPU:25, one launch (start us, length us, event | category | flops | bytes accessed | tf_op | source)
XLA Modules:
  0.0 15.1 jit_solution(5052897355371351226)
XLA Ops:
  0.7 13.6 %advect_substeps.1 = f32[3,16,32,128]{3,2,1,0:T(8,128)S(1)} custom-call(f32[3,16,32,128]{3,2,1,0:T(8,128)} %vel_hbm.1, f32[3,32,64]{2,1,0:T(8,128)} %early_hbm.1, f32[3,32,64]{2,1,0:T(8,128)} %late_hbm.1, f32[1]{0:T(128)S(6)} %copy.7.blend_ref), custom_call_target="tpu_custom_call" | custom-call | tf_op jit(solution)/shard_map/advect_substeps/pallas_call | solution.py:523
  14.3 0.9 %copy.6 = f32[3,16,32,128]{3,2,1,0:T(8,128)} copy(f32[3,16,32,128]{3,2,1,0:T(8,128)S(1)} %advect_substeps.1) | data formatting | bytes 1572864

commit v4 on v3

--- a/solution.py
+++ b/solution.py
@@ -25,6 +25,7 @@
     comps, cells_x, cells_y, cells_z = vel_hbm.shape
     share = nx // nz
     piece = early_hbm.shape[2]
+    feed_planes = -(-comps // share)
     gx, gy, gz = (lax.axis_index(name) for name in ("gx", "gy", "gz"))
     own = pl.ds(TOP, cells_y)
     first = DEPTH
@@ -40,9 +41,9 @@
         vel_hbm, cur.at[0, :, pl.ds(first, cells_x), own, :], load_sem.at[0])
     load_e = pltpu.make_async_copy(early_hbm, early, load_sem.at[1])
     load_l = pltpu.make_async_copy(late_hbm, late, load_sem.at[2])
+    load_v.start()
     load_e.start()
     load_l.start()
-    load_v.start()
 
     has_left, has_right = gx > 0, gx < nx - 1
     always = gx >= 0
@@ -68,15 +69,15 @@
     feeds = (gx != 0) & needed(gx)
 
     def gain(dx, dy, dz):
-        step = lax.div(gx + dx + 2, 2) - lax.div(gx + 2, 2)
+        step = 2 * (lax.div(gx + dx + 2, 2) - lax.div(gx + 2, 2))
         if dy:
             step = step + spanwise(dy) - gy
-        return step + 1 - 2 * gz if dz else step
+        return step + 2 - 4 * gz if dz else step
 
     barrier = pltpu.get_barrier_semaphore()
-    NEAR, FAR = 0, 1
+    HOP, WIDE, FAR = 0, 1, 2
     expected = jnp.int32(0)
-    late_expected = [jnp.int32(0), jnp.int32(0)]
+    late_expected = [jnp.int32(0)] * 3
     late_greetings = []
     soon, far = {}, {}
 
@@ -97,15 +98,16 @@
                 if place == (0, 0, 0):
                     continue
                 there, where, later = others[dx], target(*place), gain(*place)
+                kind = HOP if abs(dx) + abs(dy) + dz == 1 else WIDE
                 greet(barrier, there & (later >= 0), where)
                 beyond = top if dy == 1 else gy < 0
-                late_greetings.append((NEAR, there & (later < 0) & ~beyond, where))
+                late_greetings.append((kind, there & (later < 0) & ~beyond, where))
                 if dy == 1:
                     late_greetings.append((FAR, there & (later < 0) & beyond, where))
                 soon[place] = later <= 0
                 far[place] = (later > 0) & bottom if dy == -1 else gy < 0
                 expected = expected + jnp.where(there & soon[place], 1, 0)
-                late_expected[NEAR] = late_expected[NEAR] + jnp.where(
+                late_expected[kind] = late_expected[kind] + jnp.where(
                     there & ~soon[place] & ~far[place], 1, 0)
                 late_expected[FAR] = late_expected[FAR] + jnp.where(there & far[place], 1, 0)
     for k in range(2, nx):
@@ -123,7 +125,7 @@
     expected = expected + jnp.where(gives, jnp.where(bottom, 2, 3), 0)
     late_expected[FAR] = late_expected[FAR] + jnp.where(gives & bottom, 1, 0)
 
-    Y_UP, Y_DOWN, X, Z, FEED = range(5)
+    Y_UP, Y_DOWN, X_LEFT, X_RIGHT, Z, FEED = range(6)
     y_group = {1: Y_UP, -1: Y_DOWN}
     volume = {}
 
@@ -182,9 +184,9 @@
                 message(g, dx, dy, 1, strip_send.at[slot, rows_out(dy, reach - 1, 0), :],
                         strip_recv.at[slot, rows_in(dy, reach - 1), :]))
     x_messages = [
-        message(X, 1, 0, 0, cur.at[0, :, pl.ds(after - DEPTH, DEPTH), own, :],
+        message(X_LEFT, 1, 0, 0, cur.at[0, :, pl.ds(after - DEPTH, DEPTH), own, :],
                 cur.at[0, :, pl.ds(0, DEPTH), own, :]),
-        message(X, -1, 0, 0, cur.at[0, :, pl.ds(first, DEPTH), own, :],
+        message(X_RIGHT, -1, 0, 0, cur.at[0, :, pl.ds(first, DEPTH), own, :],
                 cur.at[0, :, pl.ds(after, DEPTH), own, :])]
     z_messages = [message(Z, 0, 0, 1, strip_send.at[pl.ds(0, comps)],
                           strip_recv.at[pl.ds(0, comps), own, :])]
@@ -193,44 +195,58 @@
         z_messages.append(
             message(Z, dx, 0, 1, strip_send.at[slot], strip_recv.at[slot, own, :]))
 
-    def feed(k, dy):
+    def feed(k, dy, whole):
         where = {"gx": 0}
         if dy:
             where["gy"] = spanwise(dy)
         src = rows_out(dy, reach, 0) if dy else pl.ds(0, cells_y)
         dst = rows_in(dy, reach) if dy else own
+        part = pl.ds(0, feed_planes) if whole else feed_planes
         return pltpu.make_async_remote_copy(
-            src_ref=feed_send.at[:, src, :], dst_ref=feed_recv.at[k, :, dst, :],
+            src_ref=feed_send.at[part, src, :], dst_ref=feed_recv.at[k, part, dst, :],
             send_sem=send_sem.at[1], recv_sem=recv_sem.at[y_group[dy] if dy else FEED],
             device_id=where, device_id_type=MESH)
 
-    def start_feed(dy, condition, ks=None):
+    def start_feed(dy, condition, ks=None, kinds=(False, True)):
         for k in ks or range(nx):
-            if k or dy:
-                pl.when((gx == k) & needed(k) & condition)(feed(k, dy).start)
-
-    def pieces(z, dy):
-        return [k for k in range(nx)
-                if (k or dy) and (k // share == z or share - z == k)]
-
-    def start(messages, phase, condition=None):
+            for whole in kinds if k or dy else ():
+                takes = k // share == gz if whole else share - gz == k
+                pl.when((gx == k) & takes & condition)(feed(k, dy, whole).start)
+
+    def fed_planes(z, local):
+        total = 0
+        for k in range(nx):
+            if local or k:
+                total += (feed_planes if k // share == z else 0) + (1 if share - z == k else 0)
+        return total
+
+    SOON = -1
+
+    def start(messages, phase):
         for place, copy in messages:
-            late = ~soon[place] & ~far[place]
-            when = others[place[0]] & (soon[place], late, far[place])[phase]
-            pl.when(when if condition is None else when & condition)(copy.start)
+            kind = HOP if sum(abs(d) for d in place) == 1 else WIDE
+            if phase == SOON:
+                when = soon[place]
+            elif phase == FAR:
+                when = far[place]
+            elif phase == kind:
+                when = ~soon[place] & ~far[place]
+            else:
+                continue
+            pl.when(others[place[0]] & when)(copy.start)
 
     def group_arrived(g, extra_left=0):
         settle_by_place(recv_sem.at[g], volume.get((g, 1), 0), volume.get((g, 0), 0),
                         volume.get((g, -1), 0), extra_left)
 
     def y_arrived(dy):
-        assert len(pieces(0, dy)) == len(pieces(1, dy))
-        group_arrived(y_group[dy], len(pieces(0, dy)) * comps * reach)
+        assert fed_planes(0, True) == fed_planes(1, True)
+        group_arrived(y_group[dy], fed_planes(0, True) * reach)
 
     def feed_arrived():
         for z in range(nz):
             pl.when(at_left & (gz == z))(
-                lambda z=z: settle(recv_sem.at[FEED], len(pieces(z, 0)) * comps * cells_y))
+                lambda z=z: settle(recv_sem.at[FEED], fed_planes(z, False) * cells_y))
 
     lane = lax.broadcasted_iota(jnp.int32, (TILE, cells_z), 1)
     group = lane // GROUP
@@ -243,12 +259,22 @@
     up_z = jnp.where(lane == 0, 0.0, COURANT)
     down_z = jnp.where(lane == cells_z - 1, 0.0, -COURANT)
 
-    with scope("load_el"):
+    def blend_piece():
         load_e.wait()
         load_l.wait()
-    weight = blend_ref[0]
-    mixed = (1.0 - weight) * early[...] + weight * late[...]
-    feed_send[...] = jnp.concatenate([mixed] * share, axis=2)
+        weight = blend_ref[0]
+        mixed = (1.0 - weight) * early[...] + weight * late[...]
+        for p in range(feed_planes):
+            feed_send[p] = jnp.concatenate(
+                [mixed[min(p * share + j, comps - 1)] for j in range(share)], axis=1)
+        for b in range(cells_y // TILE):
+            rows = slice(TILE * b, TILE * (b + 1))
+            packed = jnp.zeros((TILE, cells_z), jnp.float32)
+            for c in range(comps):
+                repeated = jnp.concatenate([mixed[c, rows]] * share, axis=1)
+                packed = jnp.where(
+                    group == c, pltpu.roll(repeated, GROUP * c + half, 1), packed)
+            feed_send[feed_planes, rows, :] = packed
 
     with scope("load_v"):
         load_v.wait()
@@ -285,24 +311,53 @@
 
     with scope("pack"):
         pack_rows([row_blocks[0], row_blocks[-1]])
+    with scope("blend"):
+        blend_piece()
+
+    @pl.when(bottom)
+    def _():
+        with scope("pack2"):
+            pack_rows(row_blocks[1:-1])
+
     with scope("barrier"):
         await_greetings(barrier, expected)
-    with scope("send"):
-        start(y_strips[1], 0)
+
+    def start_up():
+        start(y_strips[1], SOON)
         start_feed(1, always, range(2, nx))
         start_feed(1, top, range(2))
-        start(y_main[1], 0)
-        start(y_strips[-1], 0)
+        start(y_main[1], SOON)
+
+    def start_down():
+        start(y_strips[-1], SOON)
         start_feed(-1, ~bottom)
-        start(y_main[-1], 0)
-        start_feed(0, always)
-        start(x_messages, 0)
+        start(y_main[-1], SOON)
+
+    with scope("send"):
+        @pl.when(top)
+        def _():
+            start_up()
+            start_down()
+
+        @pl.when(~top)
+        def _():
+            start_down()
+            start_up()
+
+        start_feed(0, always, kinds=(False,))
         for which, condition, where in late_greetings:
             greet(late_sem.at[which], condition, where)
-    with scope("pack2"):
-        pack_rows(row_blocks[1:-1])
-    with scope("send2"):
-        start(z_messages, 0)
+
+    @pl.when(~bottom)
+    def _():
+        with scope("pack2"):
+            pack_rows(row_blocks[1:-1])
+
+    with scope("send3"):
+        start(z_messages[1:], SOON)
+        start(x_messages, SOON)
+        start_feed(0, always, kinds=(True,))
+        start(z_messages[:1], SOON)
 
     @pl.when((gx == 0) & needed(0))
     def _():
@@ -337,7 +392,7 @@
         return advance(q, behind, ahead, True)
 
     def merged(x, r, values):
-        back = lax.rem(2 * cells_z - GROUP * lax.rem(x, groups) - half, cells_z)
+        back = (2 * cells_z - GROUP * (x % groups) - half) % cells_z
         ring = strips + x // groups
         return [jnp.where(edge, pltpu.roll(cur[STEPS, c, ring, pl.ds(r, TILE), :], back, 1),
                           values[c]) for c in range(comps)]
@@ -354,7 +409,8 @@
                 for c in range(comps):
                     cur[t + 1, c, x + first, pl.ds(r, TILE), :] = values[c]
                 continue
-            values = merged(x, r, values)
+            if r in (low_rows, high_rows):
+                values = merged(x, r, values)
             for c in range(comps):
                 if r == low_rows:
                     out_ref[c, x, 0:DEPTH, :] = values[c][TILE - DEPTH:]
@@ -425,60 +481,99 @@
     def ghosts(r):
         rows = pl.ds(r, TILE)
         for c in range(comps):
-            values = feed_recv[gz * share, c, rows, :]
-            for k in range(1, share):
-                values = jnp.where(lane // piece == k,
-                                   feed_recv[gz * share + k, c, rows, :], values)
+            for k in range(share):
+                part = feed_recv[gz * share + k, c // share, rows, :]
+                if k != c % share:
+                    part = pltpu.roll(part, (k - c % share) * piece % cells_z, 1)
+                values = part if k == 0 else jnp.where(lane // piece == k, part, values)
             inflow[c, rows, :] = values
-            beyond = feed_recv[share - gz, c, rows, :]
-            there = turn(groups - 1)
-            there_values = jnp.where(mine, pltpu.roll(values, there, 1),
-                                     pltpu.roll(beyond, there, 1))
+            beyond = feed_recv[share - gz, feed_planes, rows, :]
+            there_values = jnp.where(mine, pltpu.roll(values, turn(groups - 1), 1),
+                                     pltpu.roll(beyond, GROUP * (groups - 1 - c), 1))
             fixed[c, rows, :] = jnp.where(is_first & (group == groups - 1), there_values, 0.0)
             cur[0, c, first - 1, rows, :] = jnp.where(
                 is_first, values, cur[0, c, first - 1, rows, :])
+
+    def end_ghost(r):
+        rows = pl.ds(r, TILE)
+        for c in range(comps):
             cur[0, c, after, rows, :] = jnp.where(is_last, 0.0, cur[0, c, after, rows, :])
 
-    for t in range(STEPS - 1):
+    final_blocks = range(TOP + DEPTH, TOP + cells_y - DEPTH, TILE)
+
+    def blocks_of(t):
+        return row_blocks if t < STEPS - 1 else final_blocks
+
+    for t in range(STEPS):
         with scope("A1_%d" % t):
-            planes(t, t + 1, cells_x - 1 - t, row_blocks)
-
-    with scope("late"):
-        await_greetings(late_sem.at[NEAR], late_expected[NEAR])
-        start(y_strips[1], 1)
-        start_feed(1, ~top, range(2))
-        for messages in (y_main[1], y_strips[-1], y_main[-1], z_messages, x_messages):
-            start(messages, 1)
-
-    @pl.when(bottom)
+            planes(t, t + 1, cells_x - 1 - t, blocks_of(t))
+
+    with scope("late_hop"):
+        await_greetings(late_sem.at[HOP], late_expected[HOP])
+        start_feed(1, ~top, [0])
+        for messages in (y_main[1], y_main[-1], x_messages, z_messages):
+            start(messages, HOP)
+    with scope("late_wide"):
+        await_greetings(late_sem.at[WIDE], late_expected[WIDE])
+        start(y_strips[1], WIDE)
+        start_feed(1, ~top, [1])
+        for messages in (y_main[1], y_strips[-1], y_main[-1], z_messages):
+            start(messages, WIDE)
+
+    def across():
+        @pl.when(bottom)
+        def _():
+            with scope("far"):
+                await_greetings(late_sem.at[FAR], late_expected[FAR])
+                start(y_strips[-1], FAR)
+                start_feed(-1, always)
+                start(y_main[-1], FAR)
+
+    def left_side():
+        with scope("left_wait"):
+            pl.when(has_left)(lambda: settle(recv_sem.at[X_LEFT], volume[X_LEFT, 1]))
+            feed_arrived()
+        with scope("left"):
+            for r in row_blocks:
+                ghosts(r)
+            for t in range(STEPS):
+                planes(t, t + 1 - STEPS, t + 1, blocks_of(t))
+
+    def right_side():
+        with scope("right_wait"):
+            pl.when(has_right)(lambda: settle(recv_sem.at[X_RIGHT], volume[X_RIGHT, -1]))
+        with scope("right"):
+            for r in row_blocks:
+                end_ghost(r)
+            for t in range(STEPS):
+                planes(t, cells_x - 1 - t, cells_x - 1 - t + STEPS, blocks_of(t))
+
+    @pl.when(lax.rem(gx, 2) == 0)
     def _():
-        with scope("far"):
-            await_greetings(late_sem.at[FAR], late_expected[FAR])
-            start(y_strips[-1], 2)
-            start_feed(-1, always)
-            start(y_main[-1], 2)
-
-    with scope("x_wait"):
-        group_arrived(X)
-    with scope("feed_wait"):
-        feed_arrived()
-    with scope("A2"):
-        for r in row_blocks:
-            ghosts(r)
-        for t in range(STEPS - 1):
-            beyond = STEPS - 1 - t
-            planes(t, -beyond, t + 1, row_blocks)
-            planes(t, cells_x - 1 - t, cells_x + beyond, row_blocks)
+        right_side()
+        across()
+        left_side()
+
+    @pl.when(lax.rem(gx, 2) == 1)
+    def _():
+        left_side()
+        across()
+        right_side()
+
     with scope("z_wait"):
         group_arrived(Z)
     with scope("around"):
         for r in row_blocks:
             assemble(r)
         for t in range(STEPS):
-            for r in row_blocks:
+            for r in blocks_of(t):
                 around(t, r)
-    with scope("final"):
-        planes(STEPS - 1, 0, cells_x, row_blocks)
+        for x in range(cells_x):
+            for r in final_blocks:
+                rows = pl.ds(r - TOP, TILE)
+                values = merged(x, r, [out_ref[c, x, rows, :] for c in range(comps)])
+                for c in range(comps):
+                    out_ref[c, x, rows, :] = values[c]
 
     def finish(dy):
         r = low_rows if dy > 0 else high_rows
@@ -486,6 +581,7 @@
             y_arrived(dy)
         with scope("win%d" % dy):
             ghosts(r)
+            end_ghost(r)
             assemble(r)
             for t in range(STEPS):
                 beyond = STEPS - 1 - t
@@ -506,9 +602,13 @@
         total = {dx: sum(rows for (_, d), rows in volume.items() if d == dx)
                  for dx in (-1, 0, 1)}
         settle_by_place(send_sem.at[0], total[-1], total[0], total[1])
-        fed = comps * (cells_y + 2 * reach)
-        pl.when(feeds)(lambda: settle(send_sem.at[1], fed))
-        pl.when(at_left & needed(0))(lambda: settle(send_sem.at[1], 2 * comps * reach))
+        fed = cells_y + 2 * reach
+        whole = lax.div(gx, share) == gz
+        pl.when(~at_left & whole)(lambda: settle(send_sem.at[1], feed_planes * fed))
+        pl.when(~at_left & (share - gz == gx))(lambda: settle(send_sem.at[1], fed))
+        pl.when(at_left & whole)(lambda: settle(send_sem.at[1], 2 * feed_planes * reach))
+        if share == 1:
+            pl.when(at_left & (gz == 1))(lambda: settle(send_sem.at[1], 2 * reach))
 
 
 def local(sizes, velocity, plane_early, plane_late, blend):
@@ -517,6 +617,10 @@
     groups = cells_z // GROUP
     assert nz == 2 and ny > 2 and nx % nz == 0 and cells_z == 128
     assert cells_x == 2 * groups and 2 * DEPTH == groups and cells_y % TILE == 0
+    assert TILE == 2 * DEPTH and comps <= groups
+    share = nx // nz
+    feed_planes = -(-comps // share)
+    assert plane_early.shape[2] * share == cells_z
     dma = pltpu.SemaphoreType.DMA
     padded = cells_y + 2 * TOP
     planes = cells_x + 2 * DEPTH
@@ -530,14 +634,14 @@
             pltpu.VMEM((STEPS + 1, comps, planes + 3, padded, cells_z), jnp.float32),
             pltpu.VMEM((comps + 2, cells_y, cells_z), jnp.float32),
             pltpu.VMEM((comps + 2, padded, cells_z), jnp.float32),
-            pltpu.VMEM((comps, cells_y, cells_z), jnp.float32),
-            pltpu.VMEM((nx, comps, padded, cells_z), jnp.float32),
+            pltpu.VMEM((feed_planes + 1, cells_y, cells_z), jnp.float32),
+            pltpu.VMEM((nx, feed_planes + 1, padded, cells_z), jnp.float32),
             pltpu.VMEM((comps, padded, cells_z), jnp.float32),
             pltpu.VMEM((comps, padded, cells_z), jnp.float32),
             pltpu.VMEM(plane_early.shape, jnp.float32),
             pltpu.VMEM(plane_late.shape, jnp.float32),
             pltpu.VMEM((2 * comps * planes * padded, cells_z), jnp.float32),
-            pltpu.SemaphoreType.REGULAR((2,)), dma((3,)), dma((2,)), dma((5,)),
+            pltpu.SemaphoreType.REGULAR((3,)), dma((3,)), dma((2,)), dma((6,)),
         ],
         compiler_params=pltpu.CompilerParams(collective_id=0, has_side_effects=True),
         name="advect_substeps",

time: 15.3 us -> 14.4 us (0.941)
  the two profiles are of different devices: /device:TPU:25 before, /device:TPU:4 now
where the time goes in v4:
time: 14.4 us; the launch traced here: 14.3 us
  Pallas kernels  12.7 us (88%)
  local copies, waits for them, and re-layouts  0.88 us (6%)
  between operations  0.66 us (5%)
    pallas_call x1, Pallas kernels, local(): pl.pallas_call(functools.partial(kernel, sizes), out_shape=pltpu.VMEM(vel...  12.7 us
    unnamed x1, local copies, waits for them, and re-layouts  0.88 us

profile of v4, /device:TPU:4, one launch (start us, length us, event | category | flops | bytes accessed | tf_op | source)
XLA Modules:
  0.0 14.3 jit_solution(10892939176959572743)
XLA Ops:
  0.7 12.7 %advect_substeps.1 = f32[3,16,32,128]{3,2,1,0:T(8,128)S(1)} custom-call(f32[3,16,32,128]{3,2,1,0:T(8,128)} %vel_hbm.1, f32[3,32,64]{2,1,0:T(8,128)} %early_hbm.1, f32[3,32,64]{2,1,0:T(8,128)} %late_hbm.1, f32[1]{0:T(128)S(6)} %copy.7.blend_ref), custom_call_target="tpu_custom_call" | custom-call | tf_op jit(solution)/shard_map/advect_substeps/pallas_call | solution.py:627
  13.4 0.9 %copy.6 = f32[3,16,32,128]{3,2,1,0:T(8,128)} copy(f32[3,16,32,128]{3,2,1,0:T(8,128)S(1)} %advect_substeps.1) | data formatting | bytes 1572864

commit v5 on v4

--- a/solution.py
+++ b/solution.py
@@ -41,9 +41,9 @@
         vel_hbm, cur.at[0, :, pl.ds(first, cells_x), own, :], load_sem.at[0])
     load_e = pltpu.make_async_copy(early_hbm, early, load_sem.at[1])
     load_l = pltpu.make_async_copy(late_hbm, late, load_sem.at[2])
-    load_v.start()
     load_e.start()
     load_l.start()
+    load_v.start()
 
     has_left, has_right = gx > 0, gx < nx - 1
     always = gx >= 0
@@ -71,7 +71,8 @@
     def gain(dx, dy, dz):
         step = 2 * (lax.div(gx + dx + 2, 2) - lax.div(gx + 2, 2))
         if dy:
-            step = step + spanwise(dy) - gy
+            rows = spanwise(dy) - gy
+            step = step + jnp.where(top if dy > 0 else bottom, 8 * rows, rows)
         return step + 2 - 4 * gz if dz else step
 
     barrier = pltpu.get_barrier_semaphore()
@@ -276,6 +277,8 @@
                     group == c, pltpu.roll(repeated, GROUP * c + half, 1), packed)
             feed_send[feed_planes, rows, :] = packed
 
+    with scope("blend"):
+        blend_piece()
     with scope("load_v"):
         load_v.wait()
     swap = half + gz * (cells_z - GROUP)
@@ -309,18 +312,9 @@
                     side, jnp.where(mine, outer[d][0], pltpu.roll(outer[d][1], swap, 1)),
                     pltpu.roll(outer[d][2], cells_z // 2, 1))
 
-    with scope("pack"):
-        pack_rows([row_blocks[0], row_blocks[-1]])
-    with scope("blend"):
-        blend_piece()
-
-    @pl.when(bottom)
-    def _():
-        with scope("pack2"):
-            pack_rows(row_blocks[1:-1])
-
-    with scope("barrier"):
-        await_greetings(barrier, expected)
+    def enter():
+        with scope("barrier"):
+            await_greetings(barrier, expected)
 
     def start_up():
         start(y_strips[1], SOON)
@@ -333,31 +327,55 @@
         start_feed(-1, ~bottom)
         start(y_main[-1], SOON)
 
-    with scope("send"):
-        @pl.when(top)
-        def _():
-            start_up()
-            start_down()
-
-        @pl.when(~top)
-        def _():
-            start_down()
-            start_up()
-
-        start_feed(0, always, kinds=(False,))
+    def greet_late():
         for which, condition, where in late_greetings:
             greet(late_sem.at[which], condition, where)
 
-    @pl.when(~bottom)
-    def _():
-        with scope("pack2"):
-            pack_rows(row_blocks[1:-1])
-
-    with scope("send3"):
+    def start_across():
         start(z_messages[1:], SOON)
         start(x_messages, SOON)
         start_feed(0, always, kinds=(True,))
         start(z_messages[:1], SOON)
+
+    @pl.when(bottom)
+    def _():
+        with scope("pack"):
+            pack_rows([row_blocks[0], row_blocks[-1]])
+        with scope("pack2"):
+            pack_rows(row_blocks[1:-1])
+        enter()
+        with scope("send"):
+            start_feed(0, always, kinds=(False,))
+            start_across()
+            greet_late()
+            start_up()
+            start_down()
+
+    @pl.when(~bottom)
+    def _():
+        @pl.when(top)
+        def _():
+            pack_rows(row_blocks[-1:])
+            enter()
+            start_up()
+            pack_rows(row_blocks[:1])
+            start_down()
+
+        @pl.when(~top)
+        def _():
+            pack_rows(row_blocks[:1])
+            enter()
+            start_down()
+            pack_rows(row_blocks[-1:])
+            start_up()
+
+        with scope("send"):
+            start_feed(0, always, kinds=(False,))
+            greet_late()
+        with scope("pack2"):
+            pack_rows(row_blocks[1:-1])
+        with scope("send3"):
+            start_across()
 
     @pl.when((gx == 0) & needed(0))
     def _():
@@ -520,8 +538,8 @@
         for messages in (y_main[1], y_strips[-1], y_main[-1], z_messages):
             start(messages, WIDE)
 
-    def across():
-        @pl.when(bottom)
+    def across(z):
+        @pl.when(bottom & (gz == z))
         def _():
             with scope("far"):
                 await_greetings(late_sem.at[FAR], late_expected[FAR])
@@ -534,6 +552,7 @@
             pl.when(has_left)(lambda: settle(recv_sem.at[X_LEFT], volume[X_LEFT, 1]))
             feed_arrived()
         with scope("left"):
+            pl.when(gx == 0)(lambda: across(1))
             for r in row_blocks:
                 ghosts(r)
             for t in range(STEPS):
@@ -543,6 +562,7 @@
         with scope("right_wait"):
             pl.when(has_right)(lambda: settle(recv_sem.at[X_RIGHT], volume[X_RIGHT, -1]))
         with scope("right"):
+            pl.when(gx == 1)(lambda: across(1))
             for r in row_blocks:
                 end_ghost(r)
             for t in range(STEPS):
@@ -551,14 +571,17 @@
     @pl.when(lax.rem(gx, 2) == 0)
     def _():
         right_side()
-        across()
+        across(0)
         left_side()
 
     @pl.when(lax.rem(gx, 2) == 1)
     def _():
         left_side()
-        across()
+        across(0)
         right_side()
+
+    pl.when(gx > 1)(lambda: across(1))
+
 
     with scope("z_wait"):
         group_arrived(Z)

time: 14.4 us -> 14.5 us (level)
  the two profiles are of different devices: /device:TPU:4 before, /device:TPU:25 now
where the time goes in v5:
time: 14.5 us; the launch traced here: 14.4 us
  Pallas kernels  12.8 us (88%)
  local copies, waits for them, and re-layouts  0.88 us (6%)
  between operations  0.66 us (5%)
    pallas_call x1, Pallas kernels, local(): pl.pallas_call(functools.partial(kernel, sizes), out_shape=pltpu.VMEM(vel...  12.8 us
    unnamed x1, local copies, waits for them, and re-layouts  0.88 us

profile of v5, /device:TPU:25, one launch (start us, length us, event | category | flops | bytes accessed | tf_op | source)
XLA Modules:
  0.0 14.4 jit_solution(11096740956738884020)
XLA Ops:
  0.7 12.8 %advect_substeps.1 = f32[3,16,32,128]{3,2,1,0:T(8,128)S(1)} custom-call(f32[3,16,32,128]{3,2,1,0:T(8,128)} %vel_hbm.1, f32[3,32,64]{2,1,0:T(8,128)} %early_hbm.1, f32[3,32,64]{2,1,0:T(8,128)} %late_hbm.1, f32[1]{0:T(128)S(6)} %copy.7.blend_ref), custom_call_target="tpu_custom_call" | custom-call | tf_op jit(solution)/shard_map/advect_substeps/pallas_call | solution.py:650
  13.5 0.9 %copy.6 = f32[3,16,32,128]{3,2,1,0:T(8,128)} copy(f32[3,16,32,128]{3,2,1,0:T(8,128)S(1)} %advect_substeps.1) | data formatting | bytes 1572864
